TPU v7x, 16 devices: a whole 2x2x2 slice. The times are simulated.
16 devices in a mesh: col: 2 (over z), row: 8 (over y, x, core).
Axes of the slice: x: 2, y: 2, z: 2, core: 2. Of those that a mesh axis runs over, the one named last changes fastest.
Arguments:
- inter_mask: int32 [8192, 32768], P('row', 'col')
- user_emb: bfloat16 [8192, 64], P(('row', 'col'))
- item_emb: bfloat16 [32768, 64], P(('col', 'row'))
- triples: int32 [8192, 3], replicated
Outputs:
- output 1: bfloat16 [8192, 64], P(('row', 'col'))
- output 2: bfloat16 [32768, 64], P(('col', 'row'))
- output 3: float32 [], replicated
- output 4: float32 [8192, 64], P(('row', 'col'))
- output 5: float32 [32768, 64], P(('col', 'row'))
All inputs are finite; a program needn't handle non-finite values.
Results may differ from a plain program's by a relative error of at most 0.00971148.
Values are sent between devices in bfloat16 or wider.
A program may use at most 1 GiB of HBM per device.

v0:
```python
import jax
import jax.numpy as jnp
from jax import lax
from jax.sharding import PartitionSpec as P, NamedSharding

LAYERS = 3


def solution(mesh):
    n_col = mesh.shape['col']
    n_row = mesh.shape['row']

    def local_fn(mask_blk, user_emb, item_emb, triples):
        row_idx = lax.axis_index('row')
        col_idx = lax.axis_index('col')
        user_rows = user_emb.shape[0]
        item_rows = item_emb.shape[0]
        n_batch = triples.shape[0]

        deg_user = jnp.maximum(lax.psum(jnp.sum(mask_blk, axis=1, dtype=jnp.int32), 'col'), 1)
        deg_item = jnp.maximum(lax.psum(jnp.sum(mask_blk, axis=0, dtype=jnp.int32), 'row'), 1)
        scale_user = lax.rsqrt(deg_user.astype(jnp.float32))
        scale_item = lax.rsqrt(deg_item.astype(jnp.float32))
        adj_blk = (scale_user[:, None] * mask_blk.astype(jnp.float32) * scale_item[None, :]).astype(jnp.bfloat16)

        def user_half(item_shard):
            gathered = lax.all_gather(item_shard, 'row', axis=0, tiled=True)
            partial_sum = jnp.dot(adj_blk, gathered, preferred_element_type=jnp.float32)
            return lax.psum_scatter(partial_sum, 'col', scatter_dimension=0, tiled=True)

        def item_half(user_shard):
            gathered = lax.all_gather(user_shard, 'col', axis=0, tiled=True)
            partial_sum = lax.dot_general(adj_blk, gathered, (((0,), (0,)), ((), ())), preferred_element_type=jnp.float32)
            return lax.psum_scatter(partial_sum, 'row', scatter_dimension=0, tiled=True)

        user_cur = user_emb
        item_cur = item_emb
        user_acc = user_emb.astype(jnp.float32)
        item_acc = item_emb.astype(jnp.float32)
        for _ in range(LAYERS):
            user_next = user_half(item_cur).astype(jnp.bfloat16)
            item_next = item_half(user_cur).astype(jnp.bfloat16)
            user_acc = user_acc + user_next.astype(jnp.float32)
            item_acc = item_acc + item_next.astype(jnp.float32)
            user_cur, item_cur = user_next, item_next
        user_final = (user_acc / (LAYERS + 1)).astype(jnp.bfloat16)
        item_final = (item_acc / (LAYERS + 1)).astype(jnp.bfloat16)

        user_base = (row_idx * n_col + col_idx) * user_rows
        item_base = (col_idx * n_row + row_idx) * item_rows
        local_user = triples[:, 0] - user_base
        local_pos = triples[:, 1] - item_base
        local_neg = triples[:, 2] - item_base

        def lookup_rows(emb_table, local_ids):
            is_owned = (local_ids >= 0) & (local_ids < emb_table.shape[0])
            picked = jnp.take(emb_table, jnp.clip(local_ids, 0, emb_table.shape[0] - 1), axis=0).astype(jnp.float32)
            seg_ids = jnp.where(is_owned, local_ids, emb_table.shape[0])
            return jnp.where(is_owned[:, None], picked, 0.0), seg_ids

        rows_user, seg_user = lookup_rows(user_final, local_user)
        rows_pos, seg_pos = lookup_rows(item_final, local_pos)
        rows_neg, seg_neg = lookup_rows(item_final, local_neg)
        fetched = lax.psum(jnp.concatenate([rows_user, rows_pos, rows_neg], axis=0), ('row', 'col'))
        e_user = fetched[:n_batch]
        e_pos = fetched[n_batch:2 * n_batch]
        e_neg = fetched[2 * n_batch:]
        margin = jnp.sum(e_user * e_pos, axis=1) - jnp.sum(e_user * e_neg, axis=1)
        bpr_loss = jnp.mean(jax.nn.softplus(-margin))
        loss_coef = -jax.nn.sigmoid(-margin) / n_batch
        grad_eu = loss_coef[:, None] * (e_pos - e_neg)
        grad_epos = loss_coef[:, None] * e_user
        seed_user = jax.ops.segment_sum(grad_eu, seg_user, num_segments=user_rows)
        seed_item = jax.ops.segment_sum(jnp.concatenate([grad_epos, -grad_epos], axis=0), jnp.concatenate([seg_pos, seg_neg], axis=0), num_segments=item_rows)

        src_user = seed_user / (LAYERS + 1)
        src_item = seed_item / (LAYERS + 1)
        cot_user = src_user.astype(jnp.bfloat16)
        cot_item = src_item.astype(jnp.bfloat16)
        for _ in range(LAYERS - 1):
            new_user = (src_user + user_half(cot_item)).astype(jnp.bfloat16)
            new_item = (src_item + item_half(cot_user)).astype(jnp.bfloat16)
            cot_user, cot_item = new_user, new_item
        grad_user = src_user + user_half(cot_item)
        grad_item = src_item + item_half(cot_user)
        return user_final, item_final, bpr_loss, grad_user, grad_item

    user_spec = P(('row', 'col'), None)
    item_spec = P(('col', 'row'), None)
    return jax.shard_map(local_fn, mesh=mesh, in_specs=(P('row', 'col'), user_spec, item_spec, P()), out_specs=(user_spec, item_spec, P(), user_spec, item_spec), check_vma=False)
```

profile of v0, /device:TPU:0, one launch (start us, length us, event | category | flops | bytes accessed | tf_op | source)
XLA Modules:
  0.0 1055.6 jit_solution(4641397539103162476)
XLA Ops:
  7.2 21.5 %fusion.16 = (s32[1024]{0:T(1024)S(1)}, s32[16384]{0:T(1024)}) fusion(s32[1024,16384]{1,0:T(8,128)} %param.6), kind=kLoop, calls=%fused_computation.60 | loop fusion | flops 33537024 | bytes 67178496 | tf_op jit(solution)/shard_map/reduce_sum | solution.py:20
  28.8 0.7 all-gather.7.cloned.1.call-update
  29.5 5.6 psum.21
  35.1 4.9 all_gather.37
  40.0 37.2 %all-reduce.3.cloned.1.call-done = s32[16384]{0:T(1024)} async-done(((s32[16384]{0:T(1024)}), s32[16384]{0:T(1024)}) %all-reduce.3.cloned.1.call-update) | async-done | bytes 65552 | tf_op jit(solution)/shard_map/psum | solution.py:21
  77.2 0.9 convert_rsqrt_fusion
  78.1 32.9 %multiply_convert_fusion = bf16[1024,16384]{1,0:T(8,128)(2,1)} fusion(s32[1024,16384]{1,0:T(8,128)} %param.6, f32[16384]{0:T(1024)S(1)} %convert_rsqrt_fusion, f32[1024]{0:T(1024)S(1)} %convert_rsqrt_fusion.1), kind=kLoop, calls=%fused_computation.5 | loop fusion | flops 67108864 | bytes 100732928 | tf_op jit(solution)/shard_map/convert_element_type | solution.py:24
  111.0 15.6 %fusion.24 = f32[16384,64]{0,1:T(8,128)} fusion(bf16[1024,64]{0,1:T(8,128)(2,1)S(1)} %all_gather.37, bf16[1024,16384]{1,0:T(8,128)(2,1)} %multiply_convert_fusion), kind=kOutput, calls=%fused_computation.68 | convolution fusion | flops 2147483648 | bytes 37879808 | tf_op jit(solution)/shard_map/dot_general | solution.py:33
  126.7 22.1 %fusion.18 = f32[1024,64]{0,1:T(8,128)} fusion(bf16[1024,16384]{1,0:T(8,128)(2,1)} %multiply_convert_fusion, bf16[16384,64]{0,1:T(8,128)(2,1)} %all-gather.7.cloned.1.call-done), kind=kOutput, calls=%fused_computation.62 | convolution fusion | flops 2147483648 | bytes 35913728 | tf_op jit(solution)/shard_map/dot_general | solution.py:28
  148.9 22.5 %reduce-scatter.15.cloned.1.call-done = f32[2048,64]{0,1:T(8,128)} async-done(((f32[16384,64]{0,1:T(8,128)}), f32[2048,64]{0,1:T(8,128)}) %reduce-scatter.15.cloned.1.call-update) | async-done | bytes 524304 | tf_op jit(solution)/shard_map/reduce_scatter | solution.py:34
  171.3 1.8 convert_element_type.94
  173.2 10.6 %reduce-scatter.13.cloned.1.call-done = f32[512,64]{0,1:T(8,128)} async-done(((f32[1024,64]{0,1:T(8,128)}), f32[512,64]{0,1:T(8,128)}) %reduce-scatter.13.cloned.1.call-update) | async-done | bytes 131088 | tf_op jit(solution)/shard_map/reduce_scatter | solution.py:29
  183.8 0.9 convert_element_type.92
  184.7 5.1 all_gather.39
  189.8 20.1 %all-gather.9.cloned.1.call-done = bf16[16384,64]{0,1:T(8,128)(2,1)} async-done(((bf16[2048,64]{0,1:T(8,128)(2,1)}), bf16[16384,64]{0,1:T(8,128)(2,1)}) %all-gather.9.cloned.1.call-update) | async-done | bytes 2097168 | tf_op jit(solution)/shard_map/all_gather | solution.py:27
  209.9 22.1 %fusion.19 = f32[1024,64]{0,1:T(8,128)} fusion(bf16[1024,16384]{1,0:T(8,128)(2,1)} %multiply_convert_fusion, bf16[16384,64]{0,1:T(8,128)(2,1)} %all-gather.9.cloned.1.call-done), kind=kOutput, calls=%fused_computation.63 | convolution fusion | flops 2147483648 | bytes 35913728 | tf_op jit(solution)/shard_map/dot_general | solution.py:28
  232.1 15.6 %fusion.25 = f32[16384,64]{0,1:T(8,128)} fusion(bf16[1024,64]{0,1:T(8,128)(2,1)S(1)} %all_gather.39, bf16[1024,16384]{1,0:T(8,128)(2,1)} %multiply_convert_fusion), kind=kOutput, calls=%fused_computation.69 | convolution fusion | flops 2147483648 | bytes 37879808 | tf_op jit(solution)/shard_map/dot_general | solution.py:33
  247.8 0.9 convert_element_type.95
  248.7 4.9 all_gather.41
  253.6 15.5 %fusion.26 = f32[16384,64]{0,1:T(8,128)} fusion(bf16[1024,64]{0,1:T(8,128)(2,1)S(1)} %all_gather.41, bf16[1024,16384]{1,0:T(8,128)(2,1)} %multiply_convert_fusion), kind=kOutput, calls=%fused_computation.70 | convolution fusion | flops 2147483648 | bytes 37879808 | tf_op jit(solution)/shard_map/dot_general | solution.py:33
  269.2 0.3 all-gather.11.cloned.1.call-start
  269.5 23.6 %reduce-scatter.19.cloned.1.call-done = f32[2048,64]{0,1:T(8,128)} async-done(((f32[16384,64]{0,1:T(8,128)}), f32[2048,64]{0,1:T(8,128)}) %reduce-scatter.19.cloned.1.call-update) | async-done | bytes 524304 | tf_op jit(solution)/shard_map/reduce_scatter | solution.py:34
  293.0 48.5 %reduce-scatter.23.cloned.1.call-done = f32[2048,64]{0,1:T(8,128)} async-done(((f32[16384,64]{0,1:T(8,128)}), f32[2048,64]{0,1:T(8,128)}) %reduce-scatter.23.cloned.1.call-update) | async-done | bytes 524304 | tf_op jit(solution)/shard_map/reduce_scatter | solution.py:34
  341.5 2.0 multiply_convert_fusion.1
  343.7 0.5 and_reduce_fusion.2
  344.3 0.3 copy.16
  344.6 24.0 %gather_fusion.1 = bf16[8192,64]{1,0:T(8,128)(2,1)S(1)} fusion(bf16[2048,64]{1,0:T(8,128)(2,1)S(1)} %copy.16, s32[8192]{0:T(1024)S(1)} %get-tuple-element.35), kind=kCustom, calls=%fused_computation.clone | custom fusion | bytes 2129920 | tf_op jit(solution)/shard_map/jit(_take)/gather | solution.py:57
  368.7 29.2 %gather_fusion.2 = bf16[8192,64]{1,0:T(8,128)(2,1)} fusion(bf16[2048,64]{1,0:T(8,128)(2,1)S(1)} %copy.16, s32[8192]{0:T(1024)S(1)} %get-tuple-element.37), kind=kCustom, calls=%fused_computation.1.clone | custom fusion | bytes 2129920 | tf_op jit(solution)/shard_map/jit(_take)/gather | solution.py:57
  397.9 22.1 %fusion.20 = f32[1024,64]{0,1:T(8,128)} fusion(bf16[1024,16384]{1,0:T(8,128)(2,1)} %multiply_convert_fusion, bf16[16384,64]{0,1:T(8,128)(2,1)} %all-gather.11.cloned.1.call-done), kind=kOutput, calls=%fused_computation.64 | convolution fusion | flops 2147483648 | bytes 35913728 | tf_op jit(solution)/shard_map/dot_general | solution.py:28
  420.0 0.4 all-reduce.5.cloned.1.call-start
  420.5 9.2 convert_select_fusion
  429.9 0.9 multiply_convert_fusion.3
  431.0 24.0 %gather_fusion = bf16[8192,64]{1,0:T(8,128)(2,1)S(1)} fusion(bf16[512,64]{1,0:T(8,128)(2,1)S(1)} %copy.15, s32[8192]{0:T(1024)S(1)} %broadcast_clamp_fusion), kind=kCustom, calls=%fused_computation.2 | custom fusion | bytes 2129920 | tf_op jit(solution)/shard_map/jit(_take)/gather | solution.py:57
  455.1 2.5 convert_select_fusion.2
  457.6 11.8 %pad_maximum_fusion = f32[24576,64]{1,0:T(8,128)} fusion(f32[8192,64]{1,0:T(8,128)S(1)} %copy-done, f32[8192,64]{1,0:T(8,128)} %get-tuple-element.39, f32[8192,64]{1,0:T(8,128)S(1)} %convert_select_fusion.2), kind=kLoop, calls=%fused_computation.6 | loop fusion | flops 3145728 | bytes 12582912 | tf_op jit(solution)/shard_map/concatenate | solution.py:64
  469.5 144.9 %all-reduce.5.cloned.1.call-done = f32[24576,64]{1,0:T(8,128)} async-done(((f32[24576,64]{1,0:T(8,128)}), f32[24576,64]{1,0:T(8,128)}) %all-reduce.5.cloned.1.call-update) | async-done | bytes 6291472 | tf_op jit(solution)/shard_map/psum | solution.py:64
  614.4 6.9 multiply_reduce_fusion
  621.3 0.6 negate_multiply_fusion
  621.9 48.7 %scatter_custom_fusion = f32[512,64]{1,0:T(8,128)S(1)} fusion(s32[8192]{0:T(1024)S(1)} %bitcast.33, f32[24576,64]{1,0:T(8,128)} %all-reduce.5.cloned.1.call-done, f32[8192]{0:T(1024)S(1)} %get-tuple-element.32, f32[]{:T(128)} %constant.36.clone.1), kind=kCustom, calls=%fused_computation.11 | custom fusion | flops 1572864 | bytes 8552960 | tf_op jit(solution)/shard_map/scatter-add | solution.py:73
  670.7 4.9 all_gather.45
  675.7 15.5 %fusion.28 = f32[16384,64]{0,1:T(8,128)} fusion(bf16[1024,64]{0,1:T(8,128)(2,1)S(1)} %all_gather.45, bf16[1024,16384]{1,0:T(8,128)(2,1)} %multiply_convert_fusion), kind=kOutput, calls=%fused_computation.72 | convolution fusion | flops 2147483648 | bytes 37879808 | tf_op jit(solution)/shard_map/dot_general | solution.py:33
  691.4 5.5 fusion.17
  696.9 90.7 %scatter_custom_fusion.1 = f32[2048,64]{1,0:T(8,128)S(1)} fusion(s32[16384]{0:T(1024)S(1)} %pad_add_fusion, f32[8192,64]{1,0:T(8,128)} %get-tuple-element.10, f32[]{:T(128)} %constant.76, f32[8192,64]{1,0:T(8,128)} %get-tuple-element.11, f32[]{:T(128)} %constant.36.clone.1), kind=kCustom, calls=%fused_computation.7 | custom fusion | flops 2097152 | bytes 4718600 | tf_op jit(solution)/shard_map/scatter-add | solution.py:74
  787.6 0.3 copy.19
  787.9 1.9 add_convert_fusion
  789.9 0.5 all-gather.17.cloned.1.call-update
  790.5 23.5 %all-gather.13.cloned.1.call-done = bf16[16384,64]{0,1:T(8,128)(2,1)} async-done(((bf16[2048,64]{0,1:T(8,128)(2,1)}), bf16[16384,64]{0,1:T(8,128)(2,1)}) %all-gather.13.cloned.1.call-update) | async-done | bytes 2097168 | tf_op jit(solution)/shard_map/all_gather | solution.py:27
  814.0 22.1 %fusion.21 = f32[1024,64]{0,1:T(8,128)} fusion(bf16[1024,16384]{1,0:T(8,128)(2,1)} %multiply_convert_fusion, bf16[16384,64]{0,1:T(8,128)(2,1)} %all-gather.13.cloned.1.call-done), kind=kOutput, calls=%fused_computation.65 | convolution fusion | flops 2147483648 | bytes 35913728 | tf_op jit(solution)/shard_map/dot_general | solution.py:28
  836.1 0.3 reduce-scatter.33.cloned.1.call-start
  836.4 3.7 all-gather.17.cloned.1.call-done
  840.1 22.1 %fusion.23 = f32[1024,64]{0,1:T(8,128)} fusion(bf16[1024,16384]{1,0:T(8,128)(2,1)} %multiply_convert_fusion, bf16[16384,64]{0,1:T(8,128)(2,1)} %all-gather.17.cloned.1.call-done), kind=kOutput, calls=%fused_computation.67 | convolution fusion | flops 2147483648 | bytes 35913728 | tf_op jit(solution)/shard_map/dot_general | solution.py:28
  862.3 9.9 reduce-scatter.33.cloned.1.call-done
  872.1 1.0 add_convert_fusion.2
  873.1 4.9 all_gather.43
  878.1 15.6 %fusion.27 = f32[16384,64]{0,1:T(8,128)} fusion(bf16[1024,64]{0,1:T(8,128)(2,1)S(1)} %all_gather.43, bf16[1024,16384]{1,0:T(8,128)(2,1)} %multiply_convert_fusion), kind=kOutput, calls=%fused_computation.71 | convolution fusion | flops 2147483648 | bytes 37879808 | tf_op jit(solution)/shard_map/dot_general | solution.py:33
  893.8 5.2 all_gather.47
  898.9 15.5 %fusion.29 = f32[16384,64]{0,1:T(8,128)} fusion(bf16[1024,64]{0,1:T(8,128)(2,1)S(1)} %all_gather.47, bf16[1024,16384]{1,0:T(8,128)(2,1)} %multiply_convert_fusion), kind=kOutput, calls=%fused_computation.73 | convolution fusion | flops 2147483648 | bytes 37879808 | tf_op jit(solution)/shard_map/dot_general | solution.py:33
  914.5 24.5 %reduce-scatter.27.cloned.1.call-done = f32[2048,64]{0,1:T(8,128)} async-done(((f32[16384,64]{0,1:T(8,128)}), f32[2048,64]{0,1:T(8,128)}) %reduce-scatter.27.cloned.1.call-update) | async-done | bytes 524304 | tf_op jit(solution)/shard_map/reduce_scatter | solution.py:34
  939.0 48.4 %reduce-scatter.35.cloned.1.call-done = f32[2048,64]{0,1:T(8,128)} async-done(((f32[16384,64]{0,1:T(8,128)}), f32[2048,64]{0,1:T(8,128)}) %reduce-scatter.35.cloned.1.call-update) | async-done | bytes 524304 | tf_op jit(solution)/shard_map/reduce_scatter | solution.py:34
  987.4 2.2 multiply_add_fusion
  989.7 23.9 %all-gather.15.cloned.1.call-done = bf16[16384,64]{0,1:T(8,128)(2,1)} async-done(((bf16[2048,64]{0,1:T(8,128)(2,1)}), bf16[16384,64]{0,1:T(8,128)(2,1)}) %all-gather.15.cloned.1.call-update) | async-done | bytes 2097168 | tf_op jit(solution)/shard_map/all_gather | solution.py:27
  1013.5 22.1 %fusion.22 = f32[1024,64]{0,1:T(8,128)} fusion(bf16[1024,16384]{1,0:T(8,128)(2,1)} %multiply_convert_fusion, bf16[16384,64]{0,1:T(8,128)(2,1)} %all-gather.15.cloned.1.call-done), kind=kOutput, calls=%fused_computation.66 | convolution fusion | flops 2147483648 | bytes 35913728 | tf_op jit(solution)/shard_map/dot_general | solution.py:28
  1036.3 9.3 reduce-scatter.29.cloned.1.call-done
  1045.6 1.6 multiply_add_fusion.1
  (70 shorter events, 1.9 us)
Async XLA Ops:
  7.2 27.9 %copy-start.6 = (bf16[512,64]{0,1:T(8,128)(2,1)S(1)}, bf16[512,64]{0,1:T(8,128)(2,1)}, u32[]{:S(2)}) copy-start(bf16[512,64]{0,1:T(8,128)(2,1)} %param.7) | copy-start | bytes 196612
  7.2 70.1 %all-reduce.3.cloned.1.call-start = ((), (), s32[]{:S(2)}) async-start(), calls=%async_computation.12 | async-start | bytes 131072 | tf_op jit(solution)/shard_map/psum | solution.py:21
  28.7 98.0 %all-gather.7.cloned.1.call-start = ((), (), s32[]{:S(2)}) async-start(), calls=%async_computation.13 | async-start | bytes 2359296 | tf_op jit(solution)/shard_map/all_gather | solution.py:27
  29.5 141.9 %reduce-scatter.15.cloned.1.call-start = ((), (), s32[]{:S(2)}) async-start(), calls=%async_computation.15 | async-start | bytes 4718592 | tf_op jit(solution)/shard_map/reduce_scatter | solution.py:34
  126.6 57.2 %reduce-scatter.13.cloned.1.call-start = ((), (), s32[]{:S(2)}) async-start(), calls=%async_computation.14 | async-start | bytes 393216 | tf_op jit(solution)/shard_map/reduce_scatter | solution.py:29
  148.8 61.1 %all-gather.9.cloned.1.call-start = ((), (), s32[]{:S(2)}) async-start(), calls=%async_computation.16 | async-start | bytes 2359296 | tf_op jit(solution)/shard_map/all_gather | solution.py:27
  173.1 74.6 %reduce-scatter.17.cloned.1.call-start = ((), (), s32[]{:S(2)}) async-start(), calls=%async_computation.17 | async-start | bytes 393216 | tf_op jit(solution)/shard_map/reduce_scatter | solution.py:29
  232.0 61.0 %reduce-scatter.19.cloned.1.call-start = ((), (), s32[]{:S(2)}) async-start(), calls=%async_computation.18 | async-start | bytes 4718592 | tf_op jit(solution)/shard_map/reduce_scatter | solution.py:34
  247.7 93.8 %reduce-scatter.23.cloned.1.call-start = ((), (), s32[]{:S(2)}) async-start(), calls=%async_computation.21 | async-start | bytes 4718592 | tf_op jit(solution)/shard_map/reduce_scatter | solution.py:34
  269.2 72.4 %copy-start.1 = (f32[2048,64]{0,1:T(8,128)S(1)}, f32[2048,64]{0,1:T(8,128)}, u32[]{:S(2)}) copy-start(f32[2048,64]{0,1:T(8,128)} %reduce-scatter.15.cloned.1.call-done) | copy-start | bytes 1572868
  269.2 72.4 %copy-start.3 = (bf16[2048,64]{0,1:T(8,128)(2,1)S(1)}, bf16[2048,64]{0,1:T(8,128)(2,1)}, u32[]{:S(2)}) copy-start(bf16[2048,64]{0,1:T(8,128)(2,1)} %param.8) | copy-start | bytes 786436
  269.2 74.5 %copy-start.8 = (s32[8192,3]{0,1:T(4,128)S(1)}, s32[8192,3]{0,1:T(4,128)}, u32[]{:S(2)}) copy-start(s32[8192,3]{0,1:T(4,128)} %param.9) | copy-start | bytes 294916
  269.2 128.7 %all-gather.11.cloned.1.call-start = ((), (), s32[]{:S(2)}) async-start(), calls=%async_computation.19 | async-start | bytes 2359296 | tf_op jit(solution)/shard_map/all_gather | solution.py:27
  343.6 25.1 %copy-start.2 = (bf16[2048,64]{0,1:T(8,128)(2,1)}, bf16[2048,64]{0,1:T(8,128)(2,1)S(1)}, u32[]{:S(2)}) copy-start(bf16[2048,64]{0,1:T(8,128)(2,1)S(1)} %get-tuple-element.18) | copy-start | bytes 786436
  343.6 86.3 %reduce-scatter.21.cloned.1.call-start = ((), (), s32[]{:S(2)}) async-start(), calls=%async_computation.20 | async-start | bytes 393216 | tf_op jit(solution)/shard_map/reduce_scatter | solution.py:29
  420.0 194.4 %all-reduce.5.cloned.1.call-start = ((), (), s32[]{:S(2)}) async-start(), calls=%async_computation.22 | async-start | bytes 25165824 | tf_op jit(solution)/shard_map/psum | solution.py:64
  420.5 9.4 copy-start.4
  420.5 9.4 copy-start.5
  430.8 24.2 %copy-start.7 = (bf16[512,64]{0,1:T(8,128)(2,1)}, bf16[512,64]{0,1:T(8,128)(2,1)S(1)}, u32[]{:S(2)}) copy-start(bf16[512,64]{0,1:T(8,128)(2,1)S(1)} %multiply_convert_fusion.3) | copy-start | bytes 196612
  455.1 2.5 copy-start
  469.4 318.6 %reduce-scatter.31.cloned.1.call-start = ((), (), s32[]{:S(2)}) async-start(), calls=%async_computation.28 | async-start | bytes 4718592 | tf_op jit(solution)/shard_map/reduce_scatter | solution.py:34
  691.2 122.8 %all-gather.13.cloned.1.call-start = ((), (), s32[]{:S(2)}) async-start(), calls=%async_computation.23 | async-start | bytes 2359296 | tf_op jit(solution)/shard_map/all_gather | solution.py:27
  789.9 50.2 %all-gather.17.cloned.1.call-start = ((), (), s32[]{:S(2)}) async-start(), calls=%async_computation.29 | async-start | bytes 2359296 | tf_op jit(solution)/shard_map/all_gather | solution.py:27
  790.5 71.8 %reduce-scatter.25.cloned.1.call-start = ((), (), s32[]{:S(2)}) async-start(), calls=%async_computation.24 | async-start | bytes 393216 | tf_op jit(solution)/shard_map/reduce_scatter | solution.py:29
  836.1 36.0 %reduce-scatter.33.cloned.1.call-start = ((), (), s32[]{:S(2)}) async-start(), calls=%async_computation.30 | async-start | bytes 393216 | tf_op jit(solution)/shard_map/reduce_scatter | solution.py:29
  862.2 76.9 %reduce-scatter.27.cloned.1.call-start = ((), (), s32[]{:S(2)}) async-start(), calls=%async_computation.25 | async-start | bytes 4718592 | tf_op jit(solution)/shard_map/reduce_scatter | solution.py:34
  893.7 93.7 %reduce-scatter.35.cloned.1.call-start = ((), (), s32[]{:S(2)}) async-start(), calls=%async_computation.31 | async-start | bytes 4718592 | tf_op jit(solution)/shard_map/reduce_scatter | solution.py:34
  914.5 99.0 %all-gather.15.cloned.1.call-start = ((), (), s32[]{:S(2)}) async-start(), calls=%async_computation.26 | async-start | bytes 2359296 | tf_op jit(solution)/shard_map/all_gather | solution.py:27
  989.6 56.0 %reduce-scatter.29.cloned.1.call-start = ((), (), s32[]{:S(2)}) async-start(), calls=%async_computation.27 | async-start | bytes 393216 | tf_op jit(solution)/shard_map/reduce_scatter | solution.py:29
Sparse Core Ops, SparseCore 0:
  28.8 48.3 all-reduce.2
  79.1 23.1 all-gather.6
  126.7 44.5 reduce-scatter.14
  174.0 9.7 reduce-scatter.12
  186.1 23.7 all-gather.8
  232.1 9.7 reduce-scatter.16
  247.8 45.1 reduce-scatter.18
  296.3 45.1 reduce-scatter.22
  344.0 23.7 all-gather.10
  420.1 9.7 reduce-scatter.20
  469.5 144.8 all-reduce.4
  691.3 45.3 reduce-scatter.30
  790.0 23.9 all-gather.12
  816.3 23.7 all-gather.16
  842.1 9.7 reduce-scatter.24
  862.3 9.7 reduce-scatter.32
  893.8 45.1 reduce-scatter.26
  942.2 45.1 reduce-scatter.34
  989.7 23.7 all-gather.14
  1035.8 9.7 reduce-scatter.28
where the time goes:
time: 1060 us
  waiting for transfers between devices  452 us (43%)
  other arithmetic  245 us (23%)
  matrix products  226 us (21%)
  local copies, waits for them, and re-layouts  78.2 us (7%)
  blocking collectives  35.6 us (3%)
  between operations  16.8 us (2%)
    reduce_scatter x6, waiting for transfers between devices, item_half(): return lax.psum_scatter(partial_sum, 'row', scatter_dimension=0, tiled=True)  167 us
    psum x1, waiting for transfers between devices, local_fn(): lax.psum(jnp.concatenate([rows_user, rows_pos, rows_neg], axis=0), ('row'...  145 us
    dot_general x6, matrix products, user_half(): partial_sum = jnp.dot(adj_blk, gathered, preferred_element_type=jnp.float32)  133 us
    dot_general x6, matrix products, item_half(): lax.dot_general(adj_blk, gathered, (((0,), (0,)), ((), ())), preferred_el...  93.4 us
    scatter-add x1, other arithmetic, local_fn(): jax.ops.segment_sum(jnp.concatenate([grad_epos, -grad_epos], axis=0), jnp...  90.7 us
    gather x3, local copies, waits for them, and re-layouts, lookup_rows(): jnp.take(emb_table, jnp.clip(local_ids, 0, emb_table.shape[0] - 1), axis=0)  77.3 us
    all_gather x6, waiting for transfers between devices, user_half(): gathered = lax.all_gather(item_shard, 'row', axis=0, tiled=True)  71.1 us
    scatter-add x1, other arithmetic, local_fn(): seed_user = jax.ops.segment_sum(grad_eu, seg_user, num_segments=user_rows)  48.7 us
  transfers between devices with their start and end apart: 20, of which 15 were waited for; matrix products, arithmetic and copies ran while one was open for 31% of the time, Pallas kernels for 0%

commit v1 on v0

v1 whole, which is shorter than its diff:
```python
import functools

import jax
import jax.numpy as jnp
from jax import lax
from jax.experimental import pallas as pl
from jax.experimental.pallas import tpu as pltpu
from jax.sharding import PartitionSpec as P

LAYERS = 3
MESH = pl.DeviceIdType.MESH
F32 = jnp.float32
BF16 = jnp.bfloat16
VMEM_LIMIT = 66_000_000
NT = (((1,), (1,)), ((), ()))
CHUNK = 32


class Place:
    def __init__(self):
        r = lax.axis_index('row')
        c = lax.axis_index('col')
        core = r % 2
        x = (r // 2) % 2
        y = r // 4
        self.r, self.c, self.core = r, c, core
        self.mate = r + 1 - 2 * core
        self.xn = r + 2 - 4 * x
        self.yn = r + 4 - 8 * y
        self.dg = self.xn + 4 - 8 * y
        self.zc = 1 - c
        d = 1 - 2 * core
        self.mate_x, self.mate_y, self.mate_d = self.xn + d, self.yn + d, self.dg + d

    def to_row(self, src, dst, ssem, rsem, row):
        return pltpu.make_async_remote_copy(src_ref=src, dst_ref=dst, send_sem=ssem, recv_sem=rsem, device_id={'row': row}, device_id_type=MESH)

    def to_z(self, src, dst, ssem, rsem):
        return pltpu.make_async_remote_copy(src_ref=src, dst_ref=dst, send_sem=ssem, recv_sem=rsem, device_id={'col': self.zc}, device_id_type=MESH)


def entry_barrier(pc):
    bar = pltpu.get_barrier_semaphore()
    for j in range(1, 8):
        pl.semaphore_signal(bar, inc=1, device_id={'row': (pc.r + j) % 8}, device_id_type=MESH)
    pl.semaphore_signal(bar, inc=1, device_id={'col': pc.zc}, device_id_type=MESH)
    pl.semaphore_wait(bar, 8)


class Gather:
    def __init__(self, pc, xi, ssem, rsem):
        self.pc, self.xi, self.ssem, self.rsem = pc, xi, ssem, rsem
        self.sent = []

    def _send(self, k, ref, row):
        cp = self.pc.to_row(ref, ref, self.ssem.at[k], self.rsem.at[k], row)
        cp.start()
        self.sent.append(cp)

    def _recv(self, k, ref):
        self.pc.to_row(ref, ref, self.ssem.at[k], self.rsem.at[k], self.pc.mate).wait_recv()

    def start(self):
        pc, xi = self.pc, self.xi
        own = xi.at[pc.r]
        self._send(0, own, pc.xn)
        self._send(1, own, pc.yn)
        self._send(2, own, pc.mate)

    def wait_mate(self):
        self._recv(2, self.xi.at[self.pc.mate])

    def relay(self):
        pc, xi = self.pc, self.xi
        self._recv(0, xi.at[pc.xn])
        self._send(3, xi.at[pc.xn, 0:32], pc.yn)
        self._send(5, xi.at[pc.xn], pc.mate)
        self._recv(1, xi.at[pc.yn])
        self._send(4, xi.at[pc.yn, 32:64], pc.xn)
        self._send(6, xi.at[pc.yn], pc.mate)

    def wait_mates(self):
        pc, xi = self.pc, self.xi
        self._recv(5, xi.at[pc.mate_x])
        self._recv(6, xi.at[pc.mate_y])

    def last(self):
        pc, xi = self.pc, self.xi
        self._recv(3, xi.at[pc.dg, 0:32])
        self._recv(4, xi.at[pc.dg, 32:64])
        self._send(7, xi.at[pc.dg], pc.mate)

    def finish(self):
        self._recv(7, self.xi.at[self.pc.mate_d])
        for cp in self.sent:
            cp.wait_send()
        self.sent = []


class Scatter:
    def __init__(self, pc, pi, rd, rx, ry, rz, ssem, rsem):
        self.pc, self.pi, self.rd, self.rx, self.ry, self.rz = pc, pi, rd, rx, ry, rz
        self.ssem, self.rsem = ssem, rsem
        self.sent = []

    def _send(self, k, src, dst, row):
        cp = self.pc.to_row(src, dst, self.ssem.at[k], self.rsem.at[k], row)
        cp.start()
        self.sent.append(cp)

    def _recv(self, k, ref):
        self.pc.to_row(ref, ref, self.ssem.at[k], self.rsem.at[k], self.pc.mate).wait_recv()

    def send_mate(self):
        pc = self.pc
        for k, q in enumerate((pc.mate_d, pc.mate_x, pc.mate_y, pc.mate)):
            self._send(k, self.pi.at[q], self.rd.at[k], pc.mate)

    def first(self):
        pc, pi, rd = self.pc, self.pi, self.rd
        self._recv(0, rd.at[0])
        pi[pc.dg] += rd[0]
        self._send(4, pi.at[pc.dg, 0:32], self.rx.at[1], pc.xn)
        self._send(5, pi.at[pc.dg, 32:64], self.ry.at[1], pc.yn)
        self._recv(1, rd.at[1])
        pi[pc.xn] += rd[1]
        self._send(6, pi.at[pc.xn, 0:32], self.rx.at[0], pc.xn)
        self._recv(2, rd.at[2])
        pi[pc.yn] += rd[2]
        self._send(7, pi.at[pc.yn, 32:64], self.ry.at[0], pc.yn)
        self._recv(3, rd.at[3])
        pi[pc.r] += rd[3]

    def second(self):
        pc, pi = self.pc, self.pi
        self._recv(4, self.rx.at[1])
        pi[pc.yn, 0:32] += self.rx[1]
        self._send(8, pi.at[pc.yn, 0:32], self.rz.at[0], pc.yn)
        self._recv(5, self.ry.at[1])
        pi[pc.xn, 32:64] += self.ry[1]
        self._send(9, pi.at[pc.xn, 32:64], self.rz.at[1], pc.xn)

    def result(self, emit):
        pc, pi = self.pc, self.pi
        self._recv(6, self.rx.at[0])
        self._recv(7, self.ry.at[0])
        self._recv(8, self.rz.at[0])
        emit(0, pi[pc.r, 0:32] + self.rx[0] + self.rz[0])
        self._recv(9, self.rz.at[1])
        emit(1, pi[pc.r, 32:64] + self.ry[0] + self.rz[1])
        for cp in self.sent:
            cp.wait_send()
        self.sent = []


def item_part(a, xu, pi, parity):
    x = jnp.concatenate([xu[0], xu[1]], axis=1)

    def body(j, _):
        q = 2 * j + parity
        for n in range(0, 2048, 512):
            pi[q, :, n:n + 512] = jnp.dot(x, a[q, :, n:n + 512], preferred_element_type=F32)
        return 0

    lax.fori_loop(0, 4, body, 0)


def user_part(a, xi, up, shards, first):
    if first:
        up[...] = jnp.zeros_like(up)
    for q in shards:
        for h in range(2):
            up[h] += lax.dot_general(xi[q], a[q, h * 512:(h + 1) * 512, :], NT, preferred_element_type=F32)


def propagate(pc, a, xis, xus, ups, urs, scat, gath, zs, zr, fin_u, fin_i):
    me = pc

    def z_send(ch):
        cp = me.to_z(ups[ch].at[me.zc], urs[ch], zs.at[ch, 0], zr.at[ch, 0])
        cp.start()
        return cp

    def z_sum(ch, cp):
        cp.wait()
        return ups[ch][me.c] + urs[ch][...]

    def z_share(ch, xu):
        cp = me.to_z(xu.at[me.c], xu.at[me.c], zs.at[ch, 1], zr.at[ch, 1])
        cp.start()
        return cp

    sp, sq = scat
    gp, gq = gath
    other = 1 - me.core

    item_part(a, xus[0], sq.pi, other)
    sq.send_mate()
    item_part(a, xus[0], sq.pi, me.core)
    user_part(a, xis[0], ups[0], (me.r, me.xn), True)
    sq.first()
    user_part(a, xis[0], ups[0], (me.yn, me.mate, me.mate_x, me.mate_y, me.dg, me.mate_d), False)
    cp = z_send(0)
    u1 = z_sum(0, cp)
    xus[1][me.c] = fin_u(1, u1)
    cp = z_share(0, xus[1])
    cp.wait()
    item_part(a, xus[1], sp.pi, other)
    sp.send_mate()
    sq.second()
    item_part(a, xus[1], sp.pi, me.core)

    def keep1(half, value):
        xis[1][me.r, half * 32:half * 32 + 32] = fin_i(1, half, value)

    sq.result(keep1)
    gq.start()
    user_part(a, xis[1], ups[1], (me.r,), True)
    gq.relay()
    sp.first()
    gq.wait_mate()
    user_part(a, xis[1], ups[1], (me.xn, me.yn, me.mate), False)
    gq.last()
    gq.wait_mates()
    user_part(a, xis[1], ups[1], (me.mate_x, me.mate_y, me.dg), False)
    gq.finish()
    user_part(a, xis[1], ups[1], (me.mate_d,), False)
    cp = z_send(1)
    u2 = z_sum(1, cp)
    xus[2][me.c] = fin_u(2, u2)
    cp = z_share(1, xus[2])
    cp.wait()
    item_part(a, xus[2], sq.pi, other)
    sq.send_mate()
    sp.second()
    item_part(a, xus[2], sq.pi, me.core)
    sq.first()

    def keep2(half, value):
        xis[0][me.r, half * 32:half * 32 + 32] = fin_i(2, half, value)

    sp.result(keep2)
    gp.start()
    user_part(a, xis[0], ups[0], (me.r,), True)
    gp.relay()
    gp.wait_mate()
    user_part(a, xis[0], ups[0], (me.xn, me.yn, me.mate), False)
    sq.second()
    gp.last()
    gp.wait_mates()
    user_part(a, xis[0], ups[0], (me.mate_x, me.mate_y, me.dg), False)
    gp.finish()
    user_part(a, xis[0], ups[0], (me.mate_d,), False)
    cp = z_send(0)
    u3 = z_sum(0, cp)
    fin_u(3, u3)

    def keep3(half, value):
        fin_i(3, half, value)

    sq.result(keep3)


def comm_scratch():
    dma = pltpu.SemaphoreType.DMA
    return [
        pltpu.VMEM((8, 1024, 2048), BF16),
        pltpu.VMEM((2, 8, 64, 2048), BF16),
        pltpu.VMEM((3, 2, 64, 512), BF16),
        pltpu.VMEM((2, 2, 64, 512), F32),
        pltpu.VMEM((2, 64, 512), F32),
        pltpu.VMEM((2, 8, 64, 2048), F32),
        pltpu.VMEM((2, 4, 64, 2048), F32),
        pltpu.VMEM((2, 6, 32, 2048), F32),
        dma((2, 8)), dma((2, 8)), dma((2, 10)), dma((2, 10)), dma((2, 2)), dma((2, 2)),
    ]


def comm_objects(pc, a, xi, xu, up, ur, pi, rd, rxyz, gs, gr, ss, sr, zs, zr):
    scat = [Scatter(pc, pi.at[k], rd.at[k], rxyz.at[k, 0:2], rxyz.at[k, 2:4], rxyz.at[k, 4:6], ss.at[k], sr.at[k]) for k in range(2)]
    gath = [Gather(pc, xi.at[k], gs.at[k], gr.at[k]) for k in range(2)]
    return dict(pc=pc, a=a, xis=[xi.at[0], xi.at[1]], xus=[xu.at[k] for k in range(3)], ups=[up.at[0], up.at[1]],
                urs=[ur.at[0], ur.at[1]], scat=scat, gath=gath, zs=zs, zr=zr)


def forward_kernel(m_hbm, u0, i0, eu, ei, a_hbm, *scratch):
    comm, (stage, rowacc, cacc, dpi, drecv, dfull, du, dur, su, accu, acci, msem, ds, dr, osem) = scratch[:14], scratch[14:]
    pc = Place()
    objs = comm_objects(pc, *comm)
    a, xi, xu = comm[0], comm[1], comm[2]
    zs, zr = comm[12], comm[13]

    def fetch(i):
        return pltpu.make_async_copy(m_hbm.at[pl.ds(pl.multiple_of(i * CHUNK, CHUNK), CHUNK), :], stage.at[i % 3], msem.at[i % 3])

    n_chunk = 1024 // CHUNK
    for i in range(3):
        fetch(i).start()
    xi[0, pc.r] = i0[...]
    xu[0, pc.c] = u0[...]
    accu[...] = u0[...].astype(F32)
    acci[...] = i0[...].astype(F32)
    cacc[...] = jnp.zeros_like(cacc)
    entry_barrier(pc)
    gp = objs['gath'][0]
    gp.start()
    share0 = pc.to_z(xu.at[0, pc.c], xu.at[0, pc.c], zs.at[0, 1], zr.at[0, 1])
    share0.start()

    def chunk(i, _):
        slot = i % 3
        fetch(i).wait()
        rows = pl.ds(pl.multiple_of(i * CHUNK, CHUNK), CHUNK)

        def shard(q, racc):
            for n in range(0, 2048, 512):
                m = stage[slot, :, pl.ds(pl.multiple_of(q * 2048 + n, 512), 512)]
                a[q, rows, n:n + 512] = m.astype(F32).astype(BF16)
                cacc[q, :, n:n + 512] += m[0:8] + m[8:16] + m[16:24] + m[24:32]
                racc = racc + ((m[:, 0:128] + m[:, 128:256]) + (m[:, 256:384] + m[:, 384:512]))
            return racc

        rowacc[rows, :] = lax.fori_loop(0, 8, shard, jnp.zeros((CHUNK, 128), jnp.int32))

        @pl.when(i + 3 < n_chunk)
        def _():
            fetch(i + 3).start()

        return 0

    lax.fori_loop(0, 12, chunk, 0)
    gp.relay()
    lax.fori_loop(12, 20, chunk, 0)
    gp.last()
    gp.wait_mate()
    gp.wait_mates()
    lax.fori_loop(20, n_chunk, chunk, 0)
    gp.finish()
    share0.wait()

    def fold(q, _):
        t = jnp.sum(cacc[q], axis=0, keepdims=True)
        for s in range(8):
            dpi[q, s:s + 1, :] = t[:, s * 256:(s + 1) * 256]
        return 0

    lax.fori_loop(0, 8, fold, 0)
    copies = []
    for j in range(1, 8):
        p = (pc.r + j) % 8
        copies.append(pc.to_row(dpi.at[p], drecv.at[j - 1], ds.at[0, j - 1], dr.at[0, j - 1], p))
        copies[-1].start()
    rt = jnp.sum(rowacc[...].astype(F32).T, axis=0, keepdims=True)
    du[...] = jnp.broadcast_to(rt, (8, 1024)).astype(jnp.int32)
    zc = pc.to_z(du, dur, ds.at[0, 7], dr.at[0, 7])
    zc.start()
    total = dpi[pc.r]
    for j in range(1, 8):
        copies[j - 1].wait_recv()
        total = total + drecv[j - 1]
    dfull[pc.r] = total
    back = []
    for j in range(1, 8):
        p = (pc.r + j) % 8
        back.append(pc.to_row(dfull.at[pc.r], dfull.at[pc.r], ds.at[1, j - 1], dr.at[1, j - 1], p))
        back[-1].start()
    zc.wait_recv()
    s8 = lax.rsqrt(jnp.maximum(du[...] + dur[...], 1).astype(F32))
    su[...] = jnp.broadcast_to(s8[0:1], (128, 1024)).T
    for cp in back:
        cp.wait_recv()
    for cp in copies + back + [zc]:
        cp.wait_send()

    def form(q, _):
        for s in range(8):
            si = lax.rsqrt(jnp.maximum(dfull[q, s:s + 1, :], 1).astype(F32))

            def rows_body(t, _, s=s, si=si):
                rows = pl.ds(pl.multiple_of(t * 128, 128), 128)
                sub = su[rows, :]
                scale = (jnp.concatenate([sub, sub], axis=1) * si).astype(BF16)
                a[q, rows, s * 256:(s + 1) * 256] = a[q, rows, s * 256:(s + 1) * 256] * scale
                return 0

            lax.fori_loop(0, 8, rows_body, 0)
        return 0

    lax.fori_loop(0, 8, form, 0)
    out = pltpu.make_async_copy(a, a_hbm, osem)
    out.start()

    def fin_u(k, total):
        nxt = total.astype(BF16)
        accu[...] += nxt.astype(F32)
        return nxt

    def fin_i(k, half, total):
        nxt = total.astype(BF16)
        acci[half * 32:half * 32 + 32] += nxt.astype(F32)
        return nxt

    propagate(fin_u=fin_u, fin_i=fin_i, **objs)
    eu[...] = (accu[...] / (LAYERS + 1)).astype(BF16)
    ei[...] = (acci[...] / (LAYERS + 1)).astype(BF16)
    out.wait()


def backward_kernel(a_hbm, src_u, src_i, gu, gi, *scratch):
    comm, (osem,) = scratch[:14], scratch[14:]
    pc = Place()
    objs = comm_objects(pc, *comm)
    a, xi, xu = comm[0], comm[1], comm[2]
    zs, zr = comm[12], comm[13]
    load = pltpu.make_async_copy(a_hbm, a, osem)
    load.start()
    xi[0, pc.r] = src_i[...].astype(BF16)
    xu[0, pc.c] = src_u[...].astype(BF16)
    entry_barrier(pc)
    gp = objs['gath'][0]
    gp.start()
    share0 = pc.to_z(xu.at[0, pc.c], xu.at[0, pc.c], zs.at[0, 1], zr.at[0, 1])
    share0.start()
    gp.relay()
    gp.last()
    gp.wait_mate()
    gp.wait_mates()
    gp.finish()
    share0.wait()
    load.wait()

    def fin_u(k, total):
        value = src_u[...] + total
        if k == LAYERS:
            gu[...] = value
        return value.astype(BF16)

    def fin_i(k, half, total):
        rows = slice(half * 32, half * 32 + 32)
        value = src_i[rows] + total
        if k == LAYERS:
            gi[rows] = value
        return value.astype(BF16)

    propagate(fin_u=fin_u, fin_i=fin_i, **objs)


def forward_call(mask_blk, u0, i0):
    dma = pltpu.SemaphoreType.DMA
    vm = pl.BlockSpec(memory_space=pltpu.VMEM)
    hbm = pl.BlockSpec(memory_space=pl.ANY)
    i32 = jnp.int32
    return pl.pallas_call(
        forward_kernel,
        name='forward_chains',
        out_shape=(jax.ShapeDtypeStruct((64, 512), BF16), jax.ShapeDtypeStruct((64, 2048), BF16), jax.ShapeDtypeStruct((8, 1024, 2048), BF16)),
        in_specs=[hbm, vm, vm],
        out_specs=(vm, vm, hbm),
        scratch_shapes=comm_scratch() + [
            pltpu.VMEM((3, CHUNK, 16384), i32),
            pltpu.VMEM((1024, 128), i32),
            pltpu.VMEM((8, 8, 2048), i32),
            pltpu.VMEM((8, 8, 256), i32),
            pltpu.VMEM((7, 8, 256), i32),
            pltpu.VMEM((8, 8, 256), i32),
            pltpu.VMEM((8, 1024), i32),
            pltpu.VMEM((8, 1024), i32),
            pltpu.VMEM((1024, 128), F32),
            pltpu.VMEM((64, 512), F32),
            pltpu.VMEM((64, 2048), F32),
            dma((3,)), dma((2, 8)), dma((2, 8)), dma,
        ],
        compiler_params=pltpu.CompilerParams(collective_id=0, has_side_effects=True, vmem_limit_bytes=VMEM_LIMIT),
    )(mask_blk, u0, i0)


def backward_call(a, src_u, src_i):
    dma = pltpu.SemaphoreType.DMA
    vm = pl.BlockSpec(memory_space=pltpu.VMEM)
    hbm = pl.BlockSpec(memory_space=pl.ANY)
    return pl.pallas_call(
        backward_kernel,
        name='backward_chains',
        out_shape=(jax.ShapeDtypeStruct((64, 512), F32), jax.ShapeDtypeStruct((64, 2048), F32)),
        in_specs=[hbm, vm, vm],
        out_specs=(vm, vm),
        scratch_shapes=comm_scratch() + [dma],
        compiler_params=pltpu.CompilerParams(collective_id=1, has_side_effects=True, vmem_limit_bytes=VMEM_LIMIT),
    )(a, src_u, src_i)


def solution(mesh):
    n_col = mesh.shape['col']
    n_row = mesh.shape['row']

    def local_fn(mask_blk, user_emb, item_emb, triples):
        row_idx = lax.axis_index('row')
        col_idx = lax.axis_index('col')
        user_rows = user_emb.shape[0]
        item_rows = item_emb.shape[0]
        n_batch = triples.shape[0]

        eu_t, ei_t, adj = forward_call(mask_blk, user_emb.T, item_emb.T)
        user_final, item_final = eu_t.T, ei_t.T

        user_base = (row_idx * n_col + col_idx) * user_rows
        item_base = (col_idx * n_row + row_idx) * item_rows
        local_user = triples[:, 0] - user_base
        local_pos = triples[:, 1] - item_base
        local_neg = triples[:, 2] - item_base

        def lookup_rows(emb_table, local_ids):
            is_owned = (local_ids >= 0) & (local_ids < emb_table.shape[0])
            picked = jnp.take(emb_table, jnp.clip(local_ids, 0, emb_table.shape[0] - 1), axis=0).astype(jnp.float32)
            seg_ids = jnp.where(is_owned, local_ids, emb_table.shape[0])
            return jnp.where(is_owned[:, None], picked, 0.0), seg_ids

        rows_user, seg_user = lookup_rows(user_final, local_user)
        rows_pos, seg_pos = lookup_rows(item_final, local_pos)
        rows_neg, seg_neg = lookup_rows(item_final, local_neg)
        fetched = lax.psum(jnp.concatenate([rows_user, rows_pos, rows_neg], axis=0), ('row', 'col'))
        e_user = fetched[:n_batch]
        e_pos = fetched[n_batch:2 * n_batch]
        e_neg = fetched[2 * n_batch:]
        margin = jnp.sum(e_user * e_pos, axis=1) - jnp.sum(e_user * e_neg, axis=1)
        bpr_loss = jnp.mean(jax.nn.softplus(-margin))
        loss_coef = -jax.nn.sigmoid(-margin) / n_batch
        grad_eu = loss_coef[:, None] * (e_pos - e_neg)
        grad_epos = loss_coef[:, None] * e_user
        seed_user = jax.ops.segment_sum(grad_eu, seg_user, num_segments=user_rows)
        seed_item = jax.ops.segment_sum(jnp.concatenate([grad_epos, -grad_epos], axis=0), jnp.concatenate([seg_pos, seg_neg], axis=0), num_segments=item_rows)

        src_user = seed_user / (LAYERS + 1)
        src_item = seed_item / (LAYERS + 1)
        gu_t, gi_t = backward_call(adj, src_user.T, src_item.T)
        return user_final, item_final, bpr_loss, gu_t.T, gi_t.T

    user_spec = P(('row', 'col'), None)
    item_spec = P(('col', 'row'), None)
    return jax.shard_map(local_fn, mesh=mesh, in_specs=(P('row', 'col'), user_spec, item_spec, P()), out_specs=(user_spec, item_spec, P(), user_spec, item_spec), check_vma=False)
```

time: 1060 us -> 695 us (0.66)
  waiting for transfers between devices: 452 us -> 143 us
  Pallas kernels: 0 us -> 261 us
  matrix products: 226 us -> 0 us
  other arithmetic: 245 us -> 178 us
  blocking collectives: 35.6 us -> 0 us
  local copies, waits for them, and re-layouts: 78.2 us -> 89 us
    pallas_call x0 -> x2, Pallas kernels: none -> 261 us  [the longest x1 144 us: forward_call(): pl.pallas_call(forward_kernel, name='forward_chains', out_shape=(jax.Shap...]
    dot_general x12 -> x0, matrix products: 226 us -> none  [the longest x6 133 us: user_half(): partial_sum = jnp.dot(adj_blk, gathered, preferred_element_type=jnp.float32)]
    reduce_scatter x12 -> x0, waiting for transfers between devices: 198 us -> none  [the longest x6 167 us: item_half(): return lax.psum_scatter(partial_sum, 'row', scatter_dimension=0, tiled=True)]
    all_gather x6 -> x0, waiting for transfers between devices: 71.1 us -> none  [user_half(): gathered = lax.all_gather(item_shard, 'row', axis=0, tiled=True)]
    convert_element_type x9 -> x0, other arithmetic: 42.4 us -> none  [the longest x1 32.9 us: local_fn(): (scale_user[:, None] * mask_blk.astype(jnp.float32) * scale_item[None, :]...]
    psum x1 -> x0, waiting for transfers between devices: 37.2 us -> none  [local_fn(): lax.psum(jnp.sum(mask_blk, axis=0, dtype=jnp.int32), 'row')]
    all_gather x6 -> x0, blocking collectives: 30 us -> none  [item_half(): gathered = lax.all_gather(user_shard, 'col', axis=0, tiled=True)]
    reduce_sum x1 -> x0, other arithmetic: 21.5 us -> none  [local_fn(): jnp.sum(mask_blk, axis=1, dtype=jnp.int32)]
  transfers between devices with their start and end apart: 20 -> 1, of which waited for: 15 -> 1; matrix products, arithmetic and copies ran while one was open for 31% -> 0% of each run, Pallas kernels for 0% -> 0%
where the time goes in v1:
time: 695 us; the launch traced here: 688 us
  Pallas kernels  261 us (38%)
  other arithmetic  178 us (26%)
  waiting for transfers between devices  143 us (21%)
  local copies, waits for them, and re-layouts  89 us (13%)
  between operations  16.5 us (2%)
    pallas_call x1, Pallas kernels, forward_call(): pl.pallas_call(forward_kernel, name='forward_chains', out_shape=(jax.Shap...  144 us
    psum x1, waiting for transfers between devices, local_fn(): lax.psum(jnp.concatenate([rows_user, rows_pos, rows_neg], axis=0), ('row'...  143 us
    pallas_call x1, Pallas kernels, backward_call(): pl.pallas_call(backward_kernel, name='backward_chains', out_shape=(jax.Sh...  117 us
    scatter-add x1, other arithmetic, local_fn(): jax.ops.segment_sum(jnp.concatenate([grad_epos, -grad_epos], axis=0), jnp...  90.7 us
    gather x3, local copies, waits for them, and re-layouts, lookup_rows(): jnp.take(emb_table, jnp.clip(local_ids, 0, emb_table.shape[0] - 1), axis=0)  82.5 us
    scatter-add x1, other arithmetic, local_fn(): seed_user = jax.ops.segment_sum(grad_eu, seg_user, num_segments=user_rows)  48.7 us
    concatenate x1, other arithmetic, local_fn(): jnp.concatenate([rows_user, rows_pos, rows_neg], axis=0)  14.3 us
  transfers between devices with their start and end apart: 1, of which 1 were waited for; matrix products, arithmetic and copies ran while one was open for 0% of the time, Pallas kernels for 0%

profile of v1, /device:TPU:0, one launch (start us, length us, event | category | flops | bytes accessed | tf_op | source)
XLA Modules:
  0.0 688.1 jit_solution(16314808329650502616)
XLA Ops:
  7.2 0.0 all-reduce.2.cloned.1.call-start
  7.2 1.6 and_reduce_fusion.2
  8.9 144.2 %forward_chains.1 = (bf16[64,512]{1,0:T(8,128)(2,1)}, bf16[64,2048]{1,0:T(8,128)(2,1)}, bf16[8,1024,2048]{2,1,0:T(8,128)(2,1)}) custom-call(s32[1024,16384]{1,0:T(8,128)} %m_hbm.1, bf16[64,512]{1,0:T(8,128)(2,1)} %bitcast.26, bf16[64,2048]{1,0:T(8,128)(2,1)} %bitcast.21), custom_call_target="tpu_custom_call" | custom-call | tf_op jit(solution)/shard_map/forward_chains/pallas_call | solution.py:453
  153.2 1.2 copy.16
  154.4 29.2 %gather_fusion.1 = bf16[8192,64]{1,0:T(8,128)(2,1)} fusion(bf16[2048,64]{1,0:T(8,128)(2,1)S(1)} %copy.16, s32[8192]{0:T(1024)S(1)} %get-tuple-element.35), kind=kCustom, calls=%fused_computation.clone | custom fusion | bytes 2129920 | tf_op jit(solution)/shard_map/jit(_take)/gather | solution.py:514
  183.6 0.0 copy-start.3
  183.6 29.2 %gather_fusion.2 = bf16[8192,64]{1,0:T(8,128)(2,1)} fusion(bf16[2048,64]{1,0:T(8,128)(2,1)S(1)} %copy.16, s32[8192]{0:T(1024)S(1)} %get-tuple-element.37), kind=kCustom, calls=%fused_computation.1.clone | custom fusion | bytes 2129920 | tf_op jit(solution)/shard_map/jit(_take)/gather | solution.py:514
  212.8 0.0 copy-done.3
  212.8 0.1 copy.15
  213.0 24.0 %gather_fusion = bf16[8192,64]{1,0:T(8,128)(2,1)S(1)} fusion(bf16[512,64]{1,0:T(8,128)(2,1)S(1)} %copy.15, s32[8192]{0:T(1024)S(1)} %broadcast_clamp_fusion), kind=kCustom, calls=%fused_computation.2 | custom fusion | bytes 2129920 | tf_op jit(solution)/shard_map/jit(_take)/gather | solution.py:514
  237.0 0.0 copy-start
  237.0 0.0 copy-start.1
  237.0 2.5 convert_select_fusion.2
  239.5 0.0 copy-done
  239.5 0.0 copy-done.1
  239.6 4.6 convert_select_fusion
  244.2 14.3 %pad_maximum_fusion = f32[24576,64]{1,0:T(8,128)} fusion(f32[8192,64]{1,0:T(8,128)S(1)} %get-tuple-element.38, f32[8192,64]{1,0:T(8,128)S(1)} %get-tuple-element.39, f32[8192,64]{1,0:T(8,128)S(1)} %convert_select_fusion.2), kind=kLoop, calls=%fused_computation.5 | loop fusion | flops 3145728 | bytes 12582912 | tf_op jit(solution)/shard_map/concatenate | solution.py:521
  258.5 0.0 all-reduce.2.cloned.1.call-update
  258.6 1.0 broadcast_select_fusion
  259.5 143.2 %all-reduce.2.cloned.1.call-done = f32[24576,64]{1,0:T(8,128)} async-done(((f32[24576,64]{1,0:T(8,128)}), f32[24576,64]{1,0:T(8,128)}) %all-reduce.2.cloned.1.call-update) | async-done | bytes 6291472 | tf_op jit(solution)/shard_map/psum | solution.py:521
  402.7 6.9 %multiply_reduce_fusion = (f32[8192]{0:T(1024)S(1)}, f32[8192]{0:T(1024)S(1)}) fusion(f32[24576,64]{1,0:T(8,128)} %all-reduce.2.cloned.1.call-done), kind=kLoop, calls=%fused_computation.13 | loop fusion | flops 2080768 | bytes 6356992 | tf_op jit(solution)/shard_map/reduce_sum | solution.py:525
  409.6 0.6 negate_multiply_fusion
  410.2 5.5 fusion.16
  415.7 90.7 %scatter_custom_fusion.1 = f32[2048,64]{1,0:T(8,128)S(1)} fusion(s32[16384]{0:T(1024)S(1)} %pad_add_fusion, f32[8192,64]{1,0:T(8,128)} %get-tuple-element.18, f32[]{:T(128)} %constant.71, f32[8192,64]{1,0:T(8,128)} %get-tuple-element.19, f32[]{:T(128)} %constant.22.clone.1), kind=kCustom, calls=%fused_computation.6 | custom fusion | flops 2097152 | bytes 4718600 | tf_op jit(solution)/shard_map/scatter-add | solution.py:531
  506.4 0.3 copy.19
  506.7 0.8 multiply_bitcast_fusion.src_i
  507.5 48.7 %scatter_custom_fusion = f32[512,64]{1,0:T(8,128)S(1)} fusion(s32[8192]{0:T(1024)S(1)} %bitcast.27, f32[24576,64]{1,0:T(8,128)} %all-reduce.2.cloned.1.call-done, f32[8192]{0:T(1024)S(1)} %get-tuple-element.32, f32[]{:T(128)} %constant.22.clone.1), kind=kCustom, calls=%fused_computation.10 | custom fusion | flops 1572864 | bytes 8552960 | tf_op jit(solution)/shard_map/scatter-add | solution.py:530
  556.2 0.1 copy.18
  556.4 0.7 multiply_bitcast_fusion.1.src_u
  557.0 0.0 copy-start.2
  557.0 117.1 %backward_chains.1 = (f32[64,512]{1,0:T(8,128)}, f32[64,2048]{1,0:T(8,128)}) custom-call(bf16[8,1024,2048]{2,1,0:T(8,128)(2,1)} %get-tuple-element.13.a_hbm, f32[64,512]{1,0:T(8,128)} %multiply_bitcast_fusion.1.src_u, f32[64,2048]{1,0:T(8,128)} %multiply_bitcast_fusion.src_i), custom_call_target="tpu_custom_call" | custom-call | tf_op jit(solution)/shard_map/backward_chains/pallas_call | solution.py:481
  674.8 0.6 copy.25
  675.5 0.0 copy-done.2
  675.5 0.7 copy.26
  676.2 1.6 copy.27
  677.7 1.9 copy.28
  (6 shorter events, 0.1 us)
Async XLA Ops:
  7.2 395.5 %all-reduce.2.cloned.1.call-start = ((), (), s32[]{:S(2)}) async-start(), calls=%async_computation | async-start | bytes 25165824 | tf_op jit(solution)/shard_map/psum | solution.py:521
  183.6 29.2 %copy-start.3 = (bf16[64,512]{1,0:T(8,128)(2,1)S(1)}, bf16[64,512]{1,0:T(8,128)(2,1)}, u32[]{:S(2)}) copy-start(bf16[64,512]{1,0:T(8,128)(2,1)} %get-tuple-element.11) | copy-start | bytes 196612
  237.0 2.5 copy-start
  237.0 2.5 copy-start.1
  557.0 118.4 %copy-start.2 = (bf16[64,2048]{1,0:T(8,128)(2,1)S(1)}, bf16[64,2048]{1,0:T(8,128)(2,1)}, u32[]{:S(2)}) copy-start(bf16[64,2048]{1,0:T(8,128)(2,1)} %get-tuple-element.12) | copy-start | bytes 786436
Sparse Core Ops, SparseCore 0:
  258.7 143.9 all-reduce.1

commit v2 on v0

v2 whole, which is shorter than its diff:
```python
import functools

import jax
import jax.numpy as jnp
from jax import lax
from jax.experimental import pallas as pl
from jax.experimental.pallas import tpu as pltpu
from jax.sharding import PartitionSpec as P

LAYERS = 3
MESH = pl.DeviceIdType.MESH
F32 = jnp.float32
BF16 = jnp.bfloat16
VMEM_LIMIT = 67_043_328
NT = (((1,), (1,)), ((), ()))
NONE, ONE, TWO, THREE = range(4)
D = 64
HALF = D // 2
SHARD = 2048
USERS = 512
GROUP = 128
FOLD = 256
ROWS = 8
SLOTS = 4
BATCH = 8192
ITEMS = ROWS * SHARD
LO, HI = slice(0, HALF), slice(HALF, D)


def choose(j, values):
    out = values[-1]
    for k in range(len(values) - 1):
        out = jnp.where(j == k, values[k], out)
    return out


def window(k, size):
    return pl.ds(pl.multiple_of(k * size, size), size)


class Place:
    def __init__(self):
        r = lax.axis_index('row')
        c = lax.axis_index('col')
        core = r % 2
        x = (r // 2) % 2
        y = r // 4
        self.r, self.c, self.core = r, c, core
        self.mate = r + 1 - 2 * core
        self.xn = r + 2 - 4 * x
        self.yn = r + 4 - 8 * y
        self.dg = self.xn + 4 - 8 * y
        self.zc = 1 - c
        d = 1 - 2 * core
        self.mate_x, self.mate_y, self.mate_d = self.xn + d, self.yn + d, self.dg + d

    def to_row(self, src, dst, ssem, rsem, row):
        return pltpu.make_async_remote_copy(src_ref=src, dst_ref=dst, send_sem=ssem, recv_sem=rsem, device_id={'row': row}, device_id_type=MESH)

    def to_z(self, src, dst, ssem, rsem):
        return pltpu.make_async_remote_copy(src_ref=src, dst_ref=dst, send_sem=ssem, recv_sem=rsem, device_id={'col': self.zc}, device_id_type=MESH)


def entry_barrier(pc):
    bar = pltpu.get_barrier_semaphore()
    for j in range(1, 8):
        pl.semaphore_signal(bar, inc=1, device_id={'row': (pc.r + j) % 8}, device_id_type=MESH)
    pl.semaphore_signal(bar, inc=1, device_id={'col': pc.zc}, device_id_type=MESH)
    pl.semaphore_wait(bar, 8)


class Gather:
    def __init__(self, pc, unit, part, ssem, rsem):
        self.pc, self.unit, self.part, self.ssem, self.rsem = pc, unit, part, ssem, rsem
        self.sent = []

    def _send(self, k, ref, row):
        cp = self.pc.to_row(ref, ref, self.ssem.at[k], self.rsem.at[k], row)
        cp.start()
        self.sent.append(cp)

    def _recv(self, k, ref):
        self.pc.to_row(ref, ref, self.ssem.at[k], self.rsem.at[k], self.pc.mate).wait_recv()

    def start(self):
        pc = self.pc
        own = self.unit(pc.r)
        self._send(0, own, pc.xn)
        self._send(1, own, pc.yn)
        self._send(2, own, pc.mate)

    def wait_mate(self):
        self._recv(2, self.unit(self.pc.mate))

    def relay(self):
        pc = self.pc
        self._recv(0, self.unit(pc.xn))
        self._send(3, self.part(pc.xn, 0), pc.yn)
        self._send(5, self.unit(pc.xn), pc.mate)
        self._recv(1, self.unit(pc.yn))
        self._send(4, self.part(pc.yn, 1), pc.xn)
        self._send(6, self.unit(pc.yn), pc.mate)

    def wait_mates(self):
        pc = self.pc
        self._recv(5, self.unit(pc.mate_x))
        self._recv(6, self.unit(pc.mate_y))

    def last(self):
        pc = self.pc
        self._recv(3, self.part(pc.dg, 0))
        self._recv(4, self.part(pc.dg, 1))
        self._send(7, self.unit(pc.dg), pc.mate)

    def finish(self):
        self._recv(7, self.unit(self.pc.mate_d))
        for cp in self.sent:
            cp.wait_send()
        self.sent = []


def whole_gather(pc, ref, ssem, rsem):
    half = ref.shape[1] // 2
    return Gather(pc, lambda q: ref.at[q], lambda q, h: ref.at[q, h * half:(h + 1) * half], ssem, rsem)


def lane_gather(pc, ref, lanes, ssem, rsem):
    half = ref.shape[1] // 2
    return Gather(pc, lambda q: ref.at[q, :, 0:lanes], lambda q, h: ref.at[q, h * half:(h + 1) * half, 0:lanes], ssem, rsem)


class Scatter:
    def __init__(self, pc, pi, rd, rx, ry, rz, ssem, rsem):
        self.pc, self.pi = pc, pi
        self.rd, self.rx, self.ry, self.rz = rd, rx, ry, rz
        self.ssem, self.rsem = ssem, rsem
        self.mates = (pc.mate_d, pc.mate_x, pc.mate_y, pc.mate)
        self.owns = (pc.dg, pc.xn, pc.yn, pc.r)
        hops = [(pi.at[q], rd.at[k], pc.mate) for k, q in enumerate(self.mates)]
        hops += [(pi.at[pc.dg, LO], rx.at[1], pc.xn), (pi.at[pc.dg, HI], ry.at[1], pc.yn)]
        hops += [(pi.at[pc.xn, LO], rx.at[0], pc.xn), (pi.at[pc.yn, HI], ry.at[0], pc.yn)]
        hops += [(pi.at[pc.yn, LO], rz.at[0], pc.yn), (pi.at[pc.xn, HI], rz.at[1], pc.xn)]
        self.hops = [pc.to_row(src, dst, ssem.at[k], rsem.at[k], to) for k, (src, dst, to) in enumerate(hops)]
        self.far = self.hops[4:6]
        self.near = self.hops[6:8]
        self.late = self.hops[8:]

    def item(self, a, xu, send_far=True, send_near=True, between=None):
        pc, pi = self.pc, self.pi
        x = jnp.concatenate([xu[0], xu[1]], axis=1)
        blocks = [slice(n, n + USERS) for n in range(0, SHARD, USERS)]

        def mates(j, _):
            q = choose(j, self.mates)
            for n in blocks:
                pi[q, :, n] = jnp.dot(x, a[q, :, n], preferred_element_type=F32)
            pc.to_row(pi.at[q], self.rd.at[j], self.ssem.at[j], self.rsem.at[j], pc.mate).start()
            return 0

        def owns(j, _):
            q = choose(j, self.owns)
            pc.to_row(pi.at[q], self.rd.at[j], self.ssem.at[j], self.rsem.at[j], pc.mate).wait_recv()
            for n in blocks:
                pi[q, :, n] = self.rd[j, :, n] + jnp.dot(x, a[q, :, n], preferred_element_type=F32)
            if send_far:
                @pl.when(j == 0)
                def _():
                    self.start_far()
            return 0

        lax.fori_loop(0, len(self.mates), mates, 0)
        if between is not None:
            between()
        lax.fori_loop(0, len(self.owns), owns, 0)
        if send_near:
            self.start_near()

    def start_far(self):
        for hop in self.far:
            hop.start()

    def start_near(self):
        for hop in self.near:
            hop.start()

    def second(self):
        pc, pi = self.pc, self.pi
        self.far[0].wait_recv()
        pi[pc.yn, LO] += self.rx[1]
        self.late[0].start()
        self.far[1].wait_recv()
        pi[pc.xn, HI] += self.ry[1]
        self.late[1].start()

    def result(self, emit):
        pc, pi = self.pc, self.pi
        self.near[0].wait_recv()
        self.near[1].wait_recv()
        self.late[0].wait_recv()
        emit(LO, pi[pc.r, LO] + self.rx[0] + self.rz[0])
        self.late[1].wait_recv()
        emit(HI, pi[pc.r, HI] + self.ry[0] + self.rz[1])
        for hop in self.hops:
            hop.wait_send()


def user_part(a, xi, up, shards, first=False):
    if first:
        up[...] = jnp.zeros_like(up)

    def body(j, _):
        q = choose(j, shards)
        for h in range(2):
            up[h] += lax.dot_general(xi[q], a[q, h * USERS:(h + 1) * USERS, :], NT, preferred_element_type=F32)
        return 0

    lax.fori_loop(0, len(shards), body, 0)


def user_half(a, xi, up, shards, h):
    def body(j, _):
        q = choose(j, shards)
        up[h] += lax.dot_general(xi[q], a[q, window(h, USERS), :], NT, preferred_element_type=F32)
        return 0

    lax.fori_loop(0, len(shards), body, 0)


def propagate(pc, a, xis, xus, ups, urs, scat, gath, zs, zr, fin_u, fin_i, gather_first=False, after_u3=None):
    me = pc
    sp, sq = scat
    gp, gq = gath
    near = (me.r, me.mate, me.xn, me.yn)
    far = (me.mate_x, me.mate_y, me.dg, me.mate_d)

    def users_and_send(ch, shards):
        up = ups[ch]
        user_half(a, xis[ch], up, shards, me.zc)
        cp = me.to_z(up.at[me.zc], urs[ch], zs.at[ch, 0], zr.at[ch, 0])
        cp.start()
        user_half(a, xis[ch], up, shards, me.c)
        return cp

    def z_sum(ch, cp):
        cp.wait()
        return ups[ch][me.c] + urs[ch][...]

    def z_share(ch, xu):
        cp = me.to_z(xu.at[me.c], xu.at[me.c], zs.at[ch, 1], zr.at[ch, 1])
        cp.start()
        return cp

    sq.item(a, xus[0], between=gp.relay if gather_first else None)
    if gather_first:
        gp.wait_mate()
    user_part(a, xis[0], ups[0], near, True)
    if gather_first:
        gp.last()
        gp.wait_mates()
        gp.finish()
    sq.second()
    cp = users_and_send(0, far)
    xus[1][me.c] = fin_u(1, z_sum(0, cp))
    share = z_share(0, xus[1])

    def keep1(rows, value):
        xis[1][me.r, rows] = fin_i(1, rows, value)

    sq.result(keep1)
    gq.start()
    share.wait()
    sp.item(a, xus[1], send_far=False, send_near=False)
    gq.relay()
    sp.start_far()
    sp.start_near()
    gq.wait_mate()
    user_part(a, xis[1], ups[1], near, True)
    gq.last()
    gq.wait_mates()
    user_part(a, xis[1], ups[1], far[:2])
    gq.finish()
    cp = users_and_send(1, far[2:])
    sp.second()
    xus[2][me.c] = fin_u(2, z_sum(1, cp))
    z_share(1, xus[2]).wait()
    sq.item(a, xus[2], send_near=False)

    def keep2(rows, value):
        xis[0][me.r, rows] = fin_i(2, rows, value)

    sp.result(keep2)
    gp.start()
    sq.start_near()
    user_part(a, xis[0], ups[0], near[:1], True)
    gp.relay()
    sq.second()
    gp.wait_mate()
    user_part(a, xis[0], ups[0], near[1:])
    gp.last()
    gp.wait_mates()
    user_part(a, xis[0], ups[0], far[:2])
    gp.finish()
    cp = users_and_send(0, far[2:])
    fin_u(3, z_sum(0, cp))
    if after_u3 is not None:
        after_u3()

    def keep3(rows, value):
        fin_i(3, rows, value)

    sq.result(keep3)


def comm_scratch():
    dma = pltpu.SemaphoreType.DMA
    return [
        pltpu.VMEM((ROWS, 2 * USERS, SHARD), BF16),
        pltpu.VMEM((TWO, ROWS, D, SHARD), BF16),
        pltpu.VMEM((THREE, TWO, D, USERS), BF16),
        pltpu.VMEM((TWO, TWO, D, USERS), F32),
        pltpu.VMEM((TWO, D, USERS), F32),
        pltpu.VMEM((TWO, ROWS, D, SHARD), F32),
        pltpu.VMEM((TWO, 4, D, SHARD), F32),
        pltpu.VMEM((TWO, 6, HALF, SHARD), F32),
        dma((6, ROWS)), dma((6, ROWS)), dma((TWO, 10)), dma((TWO, 10)), dma((TWO, 4)), dma((TWO, 4)),
    ]


def comm_objects(pc, a, xi, xu, up, ur, pi, rd, rxyz, gs, gr, ss, sr, zs, zr):
    scat = [Scatter(pc, pi.at[k], rd.at[k], rxyz.at[k, 0:2], rxyz.at[k, 2:4], rxyz.at[k, 4:6], ss.at[k], sr.at[k]) for k in range(2)]
    gath = [whole_gather(pc, xi.at[k], gs.at[k], gr.at[k]) for k in range(2)]
    return dict(pc=pc, a=a, xis=[xi.at[0], xi.at[1]], xus=[xu.at[k] for k in range(3)], ups=[up.at[0], up.at[1]],
                urs=[ur.at[0], ur.at[1]], scat=scat, gath=gath, zs=zs, zr=zr)


def one_hot(ids, rows):
    shape = (rows, ids.shape[1])
    wide = jnp.broadcast_to(ids.astype(jnp.int16), shape)
    return jnp.where(wide == lax.broadcasted_iota(jnp.int16, shape, 0), jnp.ones((), BF16), jnp.zeros((), BF16))


def split3(v):
    v1 = v.astype(BF16)
    rest = v - v1.astype(F32)
    v2 = rest.astype(BF16)
    v3 = (rest - v2.astype(F32)).astype(BF16)
    return jnp.concatenate([v1, v2, v3], axis=0)


def mega_kernel(m_hbm, u0, i0, ids, eu, ei, loss, gu, gi, *scratch):
    comm, rest = scratch[:14], scratch[14:]
    stage, rowacc, colacc, dpi, drecv, sib, du, dur, su, accu, acci, eall, egat, cg, msem, ds, dr = rest
    pc = Place()
    objs = comm_objects(pc, *comm)
    a, xi, xu, up, ur, pi = comm[:6]
    gs, gr = comm[8:10]
    zs, zr = comm[12:]
    xi0, xi1 = xi.at[0], xi.at[1]

    def z_share(ref, ch, k):
        cp = pc.to_z(ref, ref, zs.at[ch, k], zr.at[ch, k])
        cp.start()
        return cp

    per_shard = 2 * USERS // GROUP

    def fetch(k):
        block = m_hbm.at[window(k % per_shard, GROUP), window(k // per_shard, SHARD)]
        return pltpu.make_async_copy(block, stage.at[k % SLOTS], msem.at[k % SLOTS])

    for k in range(SLOTS):
        fetch(k).start()
    xi0[pc.r] = i0[...]
    xu[0, pc.c] = u0[...]
    accu[...] = u0[...].astype(F32)
    acci[...] = i0[...].astype(F32)
    rowacc[...] = jnp.zeros_like(rowacc)
    entry_barrier(pc)
    gp, gq = objs['gath']
    gp.start()
    share0 = z_share(xu.at[0, pc.c], 0, 1)
    strip = 2 * ROWS

    def degree_copy(j, q):
        return pc.to_row(dpi.at[q], drecv.at[j - 1, q], ds.at[j - 1], dr.at[j - 1], (pc.r + j) % ROWS)

    def shard(q, _):
        colacc[...] = jnp.zeros_like(colacc)

        def block(t, _):
            k = q * per_shard + t
            slot = k % SLOTS
            fetch(k).wait()

            def rows16(g, cols):
                here = window(g, strip)
                there = pl.ds(pl.multiple_of(t * GROUP + g * strip, strip), strip)
                racc = rowacc[there, :]
                out = []
                for n in range(0, SHARD, GROUP):
                    m = stage[slot, here, n:n + GROUP]
                    a[q, there, n:n + GROUP] = m.astype(F32).astype(BF16)
                    out.append(cols[n // GROUP] + (m[:ROWS] + m[ROWS:]))
                    racc = racc + m
                rowacc[there, :] = racc
                return tuple(out)

            lanes = range(0, SHARD, GROUP)
            cols = lax.fori_loop(0, GROUP // strip, rows16, tuple(colacc[:, n:n + GROUP] for n in lanes))
            for n, col in zip(lanes, cols):
                colacc[:, n:n + GROUP] = col

            @pl.when(k + SLOTS < ROWS * per_shard)
            def _():
                fetch(k + SLOTS).start()

            return 0

        lax.fori_loop(0, per_shard, block, 0)
        sums = jnp.sum(colacc[...], axis=0, keepdims=True)
        for s in range(ROWS):
            dpi[q, s:s + 1, :] = sums[:, s * FOLD:(s + 1) * FOLD]
        for j in range(1, ROWS):
            degree_copy(j, q).start()
        return 0

    lax.fori_loop(0, 3, shard, 0)
    gp.relay()
    lax.fori_loop(3, 5, shard, 0)
    gp.last()
    gp.wait_mate()
    gp.wait_mates()
    lax.fori_loop(5, ROWS, shard, 0)
    sums = jnp.sum(rowacc[...].astype(F32).T, axis=0, keepdims=True)
    du[...] = jnp.broadcast_to(sums, du.shape).astype(jnp.int32)
    zc = pc.to_z(du, dur, ds.at[ROWS - 1], dr.at[ROWS - 1])
    zc.start()
    gp.finish()
    share0.wait()
    zc.wait()
    scale = lax.rsqrt(jnp.maximum(du[...] + dur[...], 1).astype(F32))
    su[...] = jnp.broadcast_to(scale[:1], (GROUP, 2 * USERS)).T
    for j in range(1, ROWS):
        whole = pc.to_row(dpi, drecv.at[j - 1], ds.at[j - 1], dr.at[j - 1], (pc.r + j) % ROWS)
        whole.wait()

    def form(q, _):
        deg = dpi[q]
        for j in range(ROWS - 1):
            deg = deg + drecv[j, q]
        scale = lax.rsqrt(jnp.maximum(deg, 1).astype(F32))
        for s in range(ROWS):
            sib[:, s * FOLD:(s + 1) * FOLD] = jnp.broadcast_to(scale[s:s + 1], (ROWS, FOLD))
        tall = 4 * ROWS

        def rows32(t, _):
            rows = window(t, tall)
            sub = su[rows, :]
            for n in range(0, SHARD, GROUP):
                col = sib[:, n:n + GROUP]
                both = (sub * jnp.concatenate([col, col, col, col], axis=0)).astype(BF16)
                a[q, rows, n:n + GROUP] = a[q, rows, n:n + GROUP] * both
            return 0

        lax.fori_loop(0, 2 * USERS // tall, rows32, 0)
        return 0

    lax.fori_loop(0, ROWS, form, 0)

    def fin_u(k, total):
        nxt = total.astype(BF16)
        accu[...] += nxt.astype(F32)
        return nxt

    def fin_i(k, rows, total):
        nxt = total.astype(BF16)
        acci[rows] += nxt.astype(F32)
        return nxt

    lane_c, row_c = window(pc.c, USERS), window(pc.c, D)
    chunk = pc.r * 2 + pc.c
    role = BATCH // USERS
    pending = []
    gu_all = whole_gather(pc, eall, gs.at[2], gr.at[2])
    ge = whole_gather(pc, egat, gs.at[3], gr.at[3])

    def after_u3():
        e = (accu[...] / (LAYERS + 1)).astype(BF16)
        eu[...] = e
        eall[pc.r, row_c, :] = e
        share = z_share(eall.at[pc.r, row_c, :], 0, 1)
        share.wait()
        gu_all.start()

    propagate(fin_u=fin_u, fin_i=fin_i, after_u3=after_u3, **objs)

    e = (acci[...] / (LAYERS + 1)).astype(BF16)
    ei[...] = e
    xi1[pc.r] = e
    gq.start()

    up[0] = jnp.zeros_like(up[0])

    def diffs(shards):
        def body(j, _):
            q = choose(j, shards)
            base = pc.c * ITEMS + q * SHARD
            for h in range(2):
                pos = ids[pl.ds(role + pc.r * 2 + h, 1), :] - base
                neg = ids[pl.ds(2 * role + pc.r * 2 + h, 1), :] - base
                acc = up[0, h]
                for s in range(0, SHARD, FOLD):
                    pick = one_hot(pos - s, FOLD) - one_hot(neg - s, FOLD)
                    acc = acc + jnp.dot(xi1[q, :, s:s + FOLD], pick, preferred_element_type=F32)
                up[0, h] = acc
            return 0

        lax.fori_loop(0, len(shards), body, 0)

    def users(q, acc):
        for h in range(2):
            pick = one_hot(ids[pl.ds(chunk, 1), :] - (q * 2 + h) * USERS, USERS)
            acc = acc + jnp.dot(eall[q, h * D:(h + 1) * D, :], pick, preferred_element_type=F32)
        return acc

    gu_all.relay()
    gu_all.last()
    diffs((pc.r,))
    gq.relay()
    gu_all.wait_mate()
    gu_all.wait_mates()
    gu_all.finish()
    e_user = lax.fori_loop(0, ROWS, users, jnp.zeros((D, USERS), F32))
    egat[pc.r, row_c, :] = e_user.astype(BF16)
    z1 = z_share(egat.at[pc.r, row_c, :], 1, 1)
    gq.wait_mate()
    gq.last()
    diffs((pc.mate, pc.xn, pc.yn))
    z1.wait()
    ge.start()
    gq.wait_mates()
    gq.finish()
    diffs((pc.mate_x, pc.mate_y, pc.dg, pc.mate_d))
    part = pc.to_z(up.at[0, pc.zc], ur.at[0], zs.at[0, 0], zr.at[0, 0])
    part.start()
    ge.relay()
    ge.last()
    part.wait()
    d = up[0, pc.c] + ur[0]
    margin = jnp.sum(e_user * d, axis=0, keepdims=True)
    soft = jnp.maximum(-margin, 0.0) + jnp.log1p(jnp.exp(-jnp.abs(margin)))
    coef = -jax.nn.sigmoid(-margin) / BATCH
    row8 = window(pc.c, ROWS)
    wide = (ROWS // 2, USERS)
    cg[pc.r, row8, :] = jnp.concatenate([jnp.broadcast_to(coef, wide), jnp.broadcast_to(soft, wide)], axis=0)
    z3 = z_share(cg.at[pc.r, row8, :], 1, 3)
    pi[0, pc.r, :, lane_c] = coef * d
    z2 = z_share(pi.at[0, pc.r, :, lane_c], 1, 2)
    gv = lane_gather(pc, pi.at[0], 2 * USERS, gs.at[4], gr.at[4])
    gc = whole_gather(pc, cg, gs.at[5], gr.at[5])
    z3.wait()
    gc.start()
    z2.wait()
    gv.start()
    acc = pi.at[1]
    acc[:6] = jnp.zeros((6, D, SHARD), F32)
    ge.wait_mate()
    ge.wait_mates()
    ge.finish()
    gc.relay()
    gc.last()
    gc.wait_mate()
    gc.wait_mates()
    gc.finish()
    item_base = pc.c * ITEMS + pc.r * SHARD

    def item_grads(q, total):
        for h in range(2):
            k = q * 2 + h
            co = cg[q, h * ROWS:h * ROWS + 1, :]
            total = total + cg[q, h * ROWS + 4:h * ROWS + 5, :]
            v = split3(co * egat[q, h * D:(h + 1) * D, :].astype(F32))
            pos = ids[pl.ds(role + k, 1), :] - item_base
            neg = ids[pl.ds(2 * role + k, 1), :] - item_base
            for n in range(0, SHARD, USERS):
                picks = [one_hot(pos - b, FOLD) - one_hot(neg - b, FOLD) for b in (n, n + FOLD)]
                part_g = lax.dot_general(v, jnp.concatenate(picks, axis=0), NT, preferred_element_type=F32)
                for j in range(3):
                    acc[j, :, n:n + USERS] += part_g[j * D:(j + 1) * D]
        return total

    def user_grads(q, _):
        for h in range(2):
            w = split3(pi[0, q, :, h * USERS:(h + 1) * USERS])
            pick = one_hot(ids[pl.ds(q * 2 + h, 1), :] - chunk * USERS, USERS)
            part_g = lax.dot_general(w, pick, NT, preferred_element_type=F32)
            for j in range(3):
                acc[3 + j, :, :USERS] += part_g[j * D:(j + 1) * D]
        return 0

    total = lax.fori_loop(0, 4, item_grads, jnp.zeros((1, USERS), F32))
    gv.relay()
    total = lax.fori_loop(4, ROWS, item_grads, total)
    gv.last()
    loss[...] = jnp.broadcast_to(jnp.sum(total, axis=1, keepdims=True) / BATCH, loss.shape)
    src_i, src_u = acci, accu
    src_i[...] = ((acc[0] + acc[1]) + acc[2]) / (LAYERS + 1)
    gv.wait_mate()
    gv.wait_mates()
    gv.finish()

    objs['xis'], objs['gath'] = objs['xis'][::-1], objs['gath'][::-1]
    gp, gq = objs['gath']
    xi1[pc.r] = src_i[...].astype(BF16)
    gp.start()
    lax.fori_loop(0, ROWS, user_grads, 0)
    src_u[...] = ((acc[3, :, :USERS] + acc[4, :, :USERS]) + acc[5, :, :USERS]) / (LAYERS + 1)
    xu[0, pc.c] = src_u[...].astype(BF16)
    z_share(xu.at[0, pc.c], 0, 1).wait()

    def back_u(k, total):
        value = src_u[...] + total
        if k == LAYERS:
            gu[...] = value
        return value.astype(BF16)

    def back_i(k, rows, total):
        value = src_i[rows] + total
        if k == LAYERS:
            gi[rows] = value
        return value.astype(BF16)

    propagate(fin_u=back_u, fin_i=back_i, gather_first=True, **objs)


def mega_call(mask_blk, u0, i0, ids):
    dma = pltpu.SemaphoreType.DMA
    vm = pl.BlockSpec(memory_space=pltpu.VMEM)
    hbm = pl.BlockSpec(memory_space=pl.ANY)
    i32 = jnp.int32
    shape = jax.ShapeDtypeStruct
    return pl.pallas_call(
        mega_kernel,
        name='mega',
        out_shape=(shape((D, USERS), BF16), shape((D, SHARD), BF16), shape((ROWS, GROUP), F32), shape((D, USERS), F32), shape((D, SHARD), F32)),
        in_specs=[hbm, vm, vm, vm],
        out_specs=(vm, vm, vm, vm, vm),
        scratch_shapes=comm_scratch() + [
            pltpu.VMEM((SLOTS, GROUP, SHARD), i32),
            pltpu.VMEM((2 * USERS, GROUP), i32),
            pltpu.VMEM((ROWS, SHARD), i32),
            pltpu.VMEM((ROWS, ROWS, FOLD), i32),
            pltpu.VMEM((ROWS - 1, ROWS, ROWS, FOLD), i32),
            pltpu.VMEM((ROWS, SHARD), F32),
            pltpu.VMEM((ROWS, 2 * USERS), i32),
            pltpu.VMEM((ROWS, 2 * USERS), i32),
            pltpu.VMEM((2 * USERS, GROUP), F32),
            pltpu.VMEM((D, USERS), F32),
            pltpu.VMEM((D, SHARD), F32),
            pltpu.VMEM((ROWS, 2 * D, USERS), BF16),
            pltpu.VMEM((ROWS, 2 * D, USERS), BF16),
            pltpu.VMEM((ROWS, 2 * ROWS, USERS), F32),
            dma((SLOTS,)), dma((ROWS,)), dma((ROWS,)),
        ],
        compiler_params=pltpu.CompilerParams(collective_id=0, has_side_effects=True, vmem_limit_bytes=VMEM_LIMIT),
    )(mask_blk, u0, i0, ids)


def solution(mesh):
    def local_fn(mask_blk, user_emb, item_emb, triples):
        ids = triples.T.reshape(3 * BATCH // USERS, USERS)
        eu, ei, loss, gu, gi = mega_call(mask_blk, user_emb.T, item_emb.T, ids)
        return eu.T, ei.T, loss[0, 0], gu.T, gi.T

    user_spec = P(('row', 'col'), None)
    item_spec = P(('col', 'row'), None)
    return jax.shard_map(local_fn, mesh=mesh, in_specs=(P('row', 'col'), user_spec, item_spec, P()), out_specs=(user_spec, item_spec, P(), user_spec, item_spec), check_vma=False)
```

time: 1060 us -> 284 us (0.27)
  waiting for transfers between devices: 452 us -> 0 us
  Pallas kernels: 0 us -> 274 us
  other arithmetic: 245 us -> 0 us
  matrix products: 226 us -> 0 us
  local copies, waits for them, and re-layouts: 78.2 us -> 9.38 us
  blocking collectives: 35.6 us -> 0 us
  between operations: 16.8 us -> 0.64 us
    pallas_call x0 -> x1, Pallas kernels: none -> 274 us  [mega_call(): pl.pallas_call(mega_kernel, name='mega', out_shape=(shape((D, USERS), BF1...]
    dot_general x12 -> x0, matrix products: 226 us -> none  [the longest x6 133 us: user_half(): partial_sum = jnp.dot(adj_blk, gathered, preferred_element_type=jnp.float32)]
    reduce_scatter x12 -> x0, waiting for transfers between devices: 198 us -> none  [the longest x6 167 us: item_half(): return lax.psum_scatter(partial_sum, 'row', scatter_dimension=0, tiled=True)]
    psum x2 -> x0, waiting for transfers between devices: 182 us -> none  [the longest x1 145 us: local_fn(): lax.psum(jnp.concatenate([rows_user, rows_pos, rows_neg], axis=0), ('row'...]
    scatter-add x2 -> x0, other arithmetic: 139 us -> none  [the longest x1 90.7 us: local_fn(): jax.ops.segment_sum(jnp.concatenate([grad_epos, -grad_epos], axis=0), jnp...]
    gather x3 -> x0, local copies, waits for them, and re-layouts: 77.3 us -> none  [lookup_rows(): jnp.take(emb_table, jnp.clip(local_ids, 0, emb_table.shape[0] - 1), axis=0)]
    all_gather x6 -> x0, waiting for transfers between devices: 71.1 us -> none  [user_half(): gathered = lax.all_gather(item_shard, 'row', axis=0, tiled=True)]
    convert_element_type x9 -> x0, other arithmetic: 42.4 us -> none  [the longest x1 32.9 us: local_fn(): (scale_user[:, None] * mask_blk.astype(jnp.float32) * scale_item[None, :]...]
  transfers between devices with their start and end apart: 20 -> 0, of which waited for: 15 -> 0; matrix products, arithmetic and copies ran while one was open for 31% -> 0% of each run, Pallas kernels for 0% -> 0%
where the time goes in v2:
time: 284 us
  Pallas kernels  274 us (96%)
  local copies, waits for them, and re-layouts  9.38 us (3%)
    pallas_call x1, Pallas kernels, mega_call(): pl.pallas_call(mega_kernel, name='mega', out_shape=(shape((D, USERS), BF1...  274 us
    unnamed x4, local copies, waits for them, and re-layouts  6.58 us

profile of v2, /device:TPU:0, one launch (start us, length us, event | category | flops | bytes accessed | tf_op | source)
XLA Modules:
  0.0 284.2 jit_solution(17488638056340578721)
XLA Ops:
  0.6 1.6 reshape.13.ids
  2.2 274.1 %mega.1 = (bf16[64,512]{1,0:T(8,128)(2,1)}, bf16[64,2048]{1,0:T(8,128)(2,1)}, f32[8,128]{1,0:T(8,128)}, f32[64,512]{1,0:T(8,128)}, f32[64,2048]{1,0:T(8,128)}) custom-call(s32[1024,16384]{1,0:T(8,128)} %m_hbm.1, bf16[64,512]{1,0:T(8,128)(2,1)} %bitcast.14, bf16[64,2048]{1,0:T(8,128)(2,1)} %bitcast.9, s32[48,512]{1,0:T(8,128)} %reshape.13.ids), custom_call_target="tpu_custom_call" | custom-call | tf_op jit(solution)/shard_map/mega/pallas_call | solution.py:642
  276.4 1.2 slice.3
  277.6 1.5 copy.13
  279.0 1.7 copy.14
  280.7 1.6 copy.15
  282.3 1.9 copy.16

commit v3 on v2

--- a/solution.py
+++ b/solution.py
@@ -21,7 +21,7 @@
 GROUP = 128
 FOLD = 256
 ROWS = 8
-SLOTS = 4
+SLOTS = 12
 BATCH = 8192
 ITEMS = ROWS * SHARD
 LO, HI = slice(0, HALF), slice(HALF, D)
@@ -71,35 +71,31 @@
 
 class Gather:
     def __init__(self, pc, unit, part, ssem, rsem):
-        self.pc, self.unit, self.part, self.ssem, self.rsem = pc, unit, part, ssem, rsem
-        self.sent = []
-
-    def _send(self, k, ref, row):
-        cp = self.pc.to_row(ref, ref, self.ssem.at[k], self.rsem.at[k], row)
-        cp.start()
-        self.sent.append(cp)
+        self.pc, self.unit, self.part = pc, unit, part
+        self.ssem, self.rsem = ssem, rsem
+        own = unit(pc.r)
+        hops = [(own, pc.xn), (own, pc.yn), (own, pc.mate), (part(pc.xn, 0), pc.yn), (part(pc.yn, 1), pc.xn)]
+        hops += [(unit(pc.xn), pc.mate), (unit(pc.yn), pc.mate), (unit(pc.dg), pc.mate)]
+        self.hops = [pc.to_row(ref, ref, ssem.at[k], rsem.at[k], to) for k, (ref, to) in enumerate(hops)]
 
     def _recv(self, k, ref):
         self.pc.to_row(ref, ref, self.ssem.at[k], self.rsem.at[k], self.pc.mate).wait_recv()
 
     def start(self):
-        pc = self.pc
-        own = self.unit(pc.r)
-        self._send(0, own, pc.xn)
-        self._send(1, own, pc.yn)
-        self._send(2, own, pc.mate)
+        for hop in self.hops[:3]:
+            hop.start()
 
     def wait_mate(self):
         self._recv(2, self.unit(self.pc.mate))
 
     def relay(self):
-        pc = self.pc
+        pc, hops = self.pc, self.hops
         self._recv(0, self.unit(pc.xn))
-        self._send(3, self.part(pc.xn, 0), pc.yn)
-        self._send(5, self.unit(pc.xn), pc.mate)
+        hops[3].start()
+        hops[5].start()
         self._recv(1, self.unit(pc.yn))
-        self._send(4, self.part(pc.yn, 1), pc.xn)
-        self._send(6, self.unit(pc.yn), pc.mate)
+        hops[4].start()
+        hops[6].start()
 
     def wait_mates(self):
         pc = self.pc
@@ -110,23 +106,17 @@
         pc = self.pc
         self._recv(3, self.part(pc.dg, 0))
         self._recv(4, self.part(pc.dg, 1))
-        self._send(7, self.unit(pc.dg), pc.mate)
+        self.hops[7].start()
 
     def finish(self):
         self._recv(7, self.unit(self.pc.mate_d))
-        for cp in self.sent:
-            cp.wait_send()
-        self.sent = []
+        for hop in self.hops:
+            hop.wait_send()
 
 
 def whole_gather(pc, ref, ssem, rsem):
     half = ref.shape[1] // 2
     return Gather(pc, lambda q: ref.at[q], lambda q, h: ref.at[q, h * half:(h + 1) * half], ssem, rsem)
-
-
-def lane_gather(pc, ref, lanes, ssem, rsem):
-    half = ref.shape[1] // 2
-    return Gather(pc, lambda q: ref.at[q, :, 0:lanes], lambda q, h: ref.at[q, h * half:(h + 1) * half, 0:lanes], ssem, rsem)
 
 
 class Scatter:
@@ -150,30 +140,39 @@
         x = jnp.concatenate([xu[0], xu[1]], axis=1)
         blocks = [slice(n, n + USERS) for n in range(0, SHARD, USERS)]
 
-        def mates(j, _):
+        def for_mate(j):
             q = choose(j, self.mates)
             for n in blocks:
                 pi[q, :, n] = jnp.dot(x, a[q, :, n], preferred_element_type=F32)
             pc.to_row(pi.at[q], self.rd.at[j], self.ssem.at[j], self.rsem.at[j], pc.mate).start()
-            return 0
-
-        def owns(j, _):
+
+        def for_self(j):
             q = choose(j, self.owns)
             pc.to_row(pi.at[q], self.rd.at[j], self.ssem.at[j], self.rsem.at[j], pc.mate).wait_recv()
             for n in blocks:
                 pi[q, :, n] = self.rd[j, :, n] + jnp.dot(x, a[q, :, n], preferred_element_type=F32)
+
+        def both(j, _):
+            for_mate(j + 1)
+            if between is not None:
+                @pl.when(j == 1)
+                def _():
+                    between()
+            for_self(j)
             if send_far:
                 @pl.when(j == 0)
                 def _():
                     self.start_far()
+            if send_near:
+                for k in range(2):
+                    @pl.when(j == k + 1)
+                    def _(k=k):
+                        self.near[k].start()
             return 0
 
-        lax.fori_loop(0, len(self.mates), mates, 0)
-        if between is not None:
-            between()
-        lax.fori_loop(0, len(self.owns), owns, 0)
-        if send_near:
-            self.start_near()
+        for_mate(0)
+        lax.fori_loop(0, 3, both, 0)
+        for_self(3)
 
     def start_far(self):
         for hop in self.far:
@@ -226,29 +225,30 @@
     lax.fori_loop(0, len(shards), body, 0)
 
 
-def propagate(pc, a, xis, xus, ups, urs, scat, gath, zs, zr, fin_u, fin_i, gather_first=False, after_u3=None):
+def propagate(pc, a, xis, xus, ups, urs, scat, gath, zs, zr, fin_u, fin_i, gather_first=False):
     me = pc
     sp, sq = scat
     gp, gq = gath
     near = (me.r, me.mate, me.xn, me.yn)
     far = (me.mate_x, me.mate_y, me.dg, me.mate_d)
 
-    def users_and_send(ch, shards):
-        up = ups[ch]
-        user_half(a, xis[ch], up, shards, me.zc)
-        cp = me.to_z(up.at[me.zc], urs[ch], zs.at[ch, 0], zr.at[ch, 0])
-        cp.start()
-        user_half(a, xis[ch], up, shards, me.c)
-        return cp
-
-    def z_sum(ch, cp):
-        cp.wait()
-        return ups[ch][me.c] + urs[ch][...]
-
-    def z_share(ch, xu):
-        cp = me.to_z(xu.at[me.c], xu.at[me.c], zs.at[ch, 1], zr.at[ch, 1])
-        cp.start()
-        return cp
+    def swap(ch, h):
+        return me.to_z(ups[ch].at[h], urs[ch].at[h], zs.at[ch, h], zr.at[ch, h])
+
+    def send_users(ch, shards):
+        def body(h, _):
+            user_half(a, xis[ch], ups[ch], shards, h)
+            swap(ch, h).start()
+            return 0
+
+        lax.fori_loop(0, 2, body, 0)
+
+    def join_users(ch, k, xu):
+        for h in range(2):
+            swap(ch, h).wait()
+            nxt = fin_u(k, h, ups[ch][h] + urs[ch][h])
+            if xu is not None:
+                xu[h] = nxt
 
     sq.item(a, xus[0], between=gp.relay if gather_first else None)
     if gather_first:
@@ -259,16 +259,14 @@
         gp.wait_mates()
         gp.finish()
     sq.second()
-    cp = users_and_send(0, far)
-    xus[1][me.c] = fin_u(1, z_sum(0, cp))
-    share = z_share(0, xus[1])
+    send_users(0, far)
 
     def keep1(rows, value):
         xis[1][me.r, rows] = fin_i(1, rows, value)
 
     sq.result(keep1)
     gq.start()
-    share.wait()
+    join_users(0, 1, xus[1])
     sp.item(a, xus[1], send_far=False, send_near=False)
     gq.relay()
     sp.start_far()
@@ -279,31 +277,30 @@
     gq.wait_mates()
     user_part(a, xis[1], ups[1], far[:2])
     gq.finish()
-    cp = users_and_send(1, far[2:])
+    send_users(1, far[2:])
     sp.second()
-    xus[2][me.c] = fin_u(2, z_sum(1, cp))
-    z_share(1, xus[2]).wait()
-    sq.item(a, xus[2], send_near=False)
+    join_users(1, 2, xus[2])
 
     def keep2(rows, value):
         xis[0][me.r, rows] = fin_i(2, rows, value)
 
-    sp.result(keep2)
-    gp.start()
-    sq.start_near()
+    def next_gather():
+        sp.result(keep2)
+        gp.start()
+
+    sq.item(a, xus[2], send_near=False, between=next_gather)
     user_part(a, xis[0], ups[0], near[:1], True)
     gp.relay()
-    sq.second()
+    sq.start_near()
     gp.wait_mate()
     user_part(a, xis[0], ups[0], near[1:])
+    sq.second()
     gp.last()
     gp.wait_mates()
     user_part(a, xis[0], ups[0], far[:2])
     gp.finish()
-    cp = users_and_send(0, far[2:])
-    fin_u(3, z_sum(0, cp))
-    if after_u3 is not None:
-        after_u3()
+    send_users(0, far[2:])
+    join_users(0, 3, None)
 
     def keep3(rows, value):
         fin_i(3, rows, value)
@@ -318,15 +315,14 @@
         pltpu.VMEM((TWO, ROWS, D, SHARD), BF16),
         pltpu.VMEM((THREE, TWO, D, USERS), BF16),
         pltpu.VMEM((TWO, TWO, D, USERS), F32),
-        pltpu.VMEM((TWO, D, USERS), F32),
-        pltpu.VMEM((TWO, ROWS, D, SHARD), F32),
+        pltpu.VMEM((TWO, TWO, D, USERS), F32),
         pltpu.VMEM((TWO, 4, D, SHARD), F32),
         pltpu.VMEM((TWO, 6, HALF, SHARD), F32),
-        dma((6, ROWS)), dma((6, ROWS)), dma((TWO, 10)), dma((TWO, 10)), dma((TWO, 4)), dma((TWO, 4)),
+        dma((5, ROWS)), dma((5, ROWS)), dma((TWO, 10)), dma((TWO, 10)), dma((TWO, 4)), dma((TWO, 4)),
     ]
 
 
-def comm_objects(pc, a, xi, xu, up, ur, pi, rd, rxyz, gs, gr, ss, sr, zs, zr):
+def comm_objects(pc, pi, a, xi, xu, up, ur, rd, rxyz, gs, gr, ss, sr, zs, zr):
     scat = [Scatter(pc, pi.at[k], rd.at[k], rxyz.at[k, 0:2], rxyz.at[k, 2:4], rxyz.at[k, 4:6], ss.at[k], sr.at[k]) for k in range(2)]
     gath = [whole_gather(pc, xi.at[k], gs.at[k], gr.at[k]) for k in range(2)]
     return dict(pc=pc, a=a, xis=[xi.at[0], xi.at[1]], xus=[xu.at[k] for k in range(3)], ups=[up.at[0], up.at[1]],
@@ -348,19 +344,34 @@
 
 
 def mega_kernel(m_hbm, u0, i0, ids, eu, ei, loss, gu, gi, *scratch):
-    comm, rest = scratch[:14], scratch[14:]
-    stage, rowacc, colacc, dpi, drecv, sib, du, dur, su, accu, acci, eall, egat, cg, msem, ds, dr = rest
+    comm, rest = scratch[:13], scratch[13:]
     pc = Place()
-    objs = comm_objects(pc, *comm)
-    a, xi, xu, up, ur, pi = comm[:6]
-    gs, gr = comm[8:10]
-    zs, zr = comm[12:]
-    xi0, xi1 = xi.at[0], xi.at[1]
-
-    def z_share(ref, ch, k):
-        cp = pc.to_z(ref, ref, zs.at[ch, k], zr.at[ch, k])
-        cp.start()
-        return cp
+    i32 = jnp.int32
+
+    def first(stage, rowacc, colacc, sib, su, msem):
+        form_adjacency(pc, m_hbm, u0, i0, comm, rest, stage, rowacc, colacc, sib, su, msem)
+
+    pl.run_scoped(
+        first,
+        pltpu.VMEM((SLOTS, GROUP, SHARD), i32), pltpu.VMEM((2 * USERS, GROUP), i32), pltpu.VMEM((ROWS, SHARD), i32),
+        pltpu.VMEM((ROWS, SHARD), F32), pltpu.VMEM((2 * USERS, GROUP), F32), pltpu.SemaphoreType.DMA((SLOTS,)),
+    )
+    pl.run_scoped(lambda pi: chains(pc, pi, ids, eu, ei, loss, gu, gi, comm, rest), pltpu.VMEM((TWO, ROWS, D, SHARD), F32))
+
+
+def z_share(pc, ref, ssem, rsem):
+    cp = pc.to_z(ref, ref, ssem, rsem)
+    cp.start()
+    return cp
+
+
+def form_adjacency(pc, m_hbm, u0, i0, comm, rest, stage, rowacc, colacc, sib, su, msem):
+    dpi, drecv, du, dur, accu, acci = rest[:6]
+    ds, dr = rest[-2:]
+    a, xi, xu = comm[:3]
+    zs, zr = comm[11:]
+    xi0 = xi.at[0]
+    gp = whole_gather(pc, xi0, comm[7].at[0], comm[8].at[0])
 
     per_shard = 2 * USERS // GROUP
 
@@ -372,13 +383,11 @@
         fetch(k).start()
     xi0[pc.r] = i0[...]
     xu[0, pc.c] = u0[...]
-    accu[...] = u0[...].astype(F32)
     acci[...] = i0[...].astype(F32)
     rowacc[...] = jnp.zeros_like(rowacc)
     entry_barrier(pc)
-    gp, gq = objs['gath']
     gp.start()
-    share0 = z_share(xu.at[0, pc.c], 0, 1)
+    share0 = z_share(pc, xu.at[0, pc.c], zs.at[0, 3], zr.at[0, 3])
     strip = 2 * ROWS
 
     def degree_copy(j, q):
@@ -437,6 +446,7 @@
     zc.start()
     gp.finish()
     share0.wait()
+    accu[...] = xu[0].astype(F32)
     zc.wait()
     scale = lax.rsqrt(jnp.maximum(du[...] + dur[...], 1).astype(F32))
     su[...] = jnp.broadcast_to(scale[:1], (GROUP, 2 * USERS)).T
@@ -451,25 +461,44 @@
         scale = lax.rsqrt(jnp.maximum(deg, 1).astype(F32))
         for s in range(ROWS):
             sib[:, s * FOLD:(s + 1) * FOLD] = jnp.broadcast_to(scale[s:s + 1], (ROWS, FOLD))
-        tall = 4 * ROWS
-
-        def rows32(t, _):
+        tall = ROWS * ROWS
+
+        def rows64(t, _):
             rows = window(t, tall)
             sub = su[rows, :]
             for n in range(0, SHARD, GROUP):
                 col = sib[:, n:n + GROUP]
-                both = (sub * jnp.concatenate([col, col, col, col], axis=0)).astype(BF16)
+                both = (sub * jnp.concatenate([col] * ROWS, axis=0)).astype(BF16)
                 a[q, rows, n:n + GROUP] = a[q, rows, n:n + GROUP] * both
             return 0
 
-        lax.fori_loop(0, 2 * USERS // tall, rows32, 0)
+        lax.fori_loop(0, 2 * USERS // tall, rows64, 0)
         return 0
 
     lax.fori_loop(0, ROWS, form, 0)
 
-    def fin_u(k, total):
+
+def pack_rows(x):
+    return jnp.concatenate([row[:, n:n + GROUP] for row in x for n in range(0, USERS, GROUP)], axis=0)
+
+
+def unpack_row(tile, h):
+    rows = USERS // GROUP
+    return jnp.concatenate([tile[k:k + 1] for k in range(h * rows, (h + 1) * rows)], axis=1)
+
+
+def chains(pc, pi, ids, eu, ei, loss, gu, gi, comm, rest):
+    _, _, _, _, accu, acci, eall, egat, cg, mg, ds, dr = rest
+    objs = comm_objects(pc, pi, *comm)
+    a, xi, xu, up, ur, rd = comm[:6]
+    gs, gr = comm[7:9]
+    zs, zr = comm[11:]
+    xi1 = xi.at[1]
+    gp, gq = objs['gath']
+
+    def fin_u(k, h, total):
         nxt = total.astype(BF16)
-        accu[...] += nxt.astype(F32)
+        accu[h] += nxt.astype(F32)
         return nxt
 
     def fin_i(k, rows, total):
@@ -477,29 +506,23 @@
         acci[rows] += nxt.astype(F32)
         return nxt
 
-    lane_c, row_c = window(pc.c, USERS), window(pc.c, D)
-    chunk = pc.r * 2 + pc.c
     role = BATCH // USERS
-    pending = []
     gu_all = whole_gather(pc, eall, gs.at[2], gr.at[2])
     ge = whole_gather(pc, egat, gs.at[3], gr.at[3])
-
-    def after_u3():
-        e = (accu[...] / (LAYERS + 1)).astype(BF16)
-        eu[...] = e
-        eall[pc.r, row_c, :] = e
-        share = z_share(eall.at[pc.r, row_c, :], 0, 1)
-        share.wait()
-        gu_all.start()
-
-    propagate(fin_u=fin_u, fin_i=fin_i, after_u3=after_u3, **objs)
+    propagate(fin_u=fin_u, fin_i=fin_i, **objs)
 
     e = (acci[...] / (LAYERS + 1)).astype(BF16)
-    ei[...] = e
     xi1[pc.r] = e
     gq.start()
-
-    up[0] = jnp.zeros_like(up[0])
+    ei[...] = e
+    for h in range(2):
+        eall[pc.r, h * D:(h + 1) * D, :] = (accu[h] / (LAYERS + 1)).astype(BF16)
+    gu_all.start()
+    eu[...] = (accu[pc.c] / (LAYERS + 1)).astype(BF16)
+
+    dif, eus = up.at[0], up.at[1]
+    dif[...] = jnp.zeros_like(dif)
+    eus[...] = jnp.zeros_like(eus)
 
     def diffs(shards):
         def body(j, _):
@@ -508,78 +531,87 @@
             for h in range(2):
                 pos = ids[pl.ds(role + pc.r * 2 + h, 1), :] - base
                 neg = ids[pl.ds(2 * role + pc.r * 2 + h, 1), :] - base
-                acc = up[0, h]
+                acc = dif[h]
                 for s in range(0, SHARD, FOLD):
                     pick = one_hot(pos - s, FOLD) - one_hot(neg - s, FOLD)
                     acc = acc + jnp.dot(xi1[q, :, s:s + FOLD], pick, preferred_element_type=F32)
-                up[0, h] = acc
+                dif[h] = acc
             return 0
 
         lax.fori_loop(0, len(shards), body, 0)
 
-    def users(q, acc):
-        for h in range(2):
-            pick = one_hot(ids[pl.ds(chunk, 1), :] - (q * 2 + h) * USERS, USERS)
-            acc = acc + jnp.dot(eall[q, h * D:(h + 1) * D, :], pick, preferred_element_type=F32)
-        return acc
-
-    gu_all.relay()
-    gu_all.last()
+    def users(q, _):
+        for t in range(2):
+            acc = eus[t]
+            for h in range(2):
+                pick = one_hot(ids[pl.ds(pc.r * 2 + t, 1), :] - (q * 2 + h) * USERS, USERS)
+                acc = acc + jnp.dot(eall[q, h * D:(h + 1) * D, :], pick, preferred_element_type=F32)
+            eus[t] = acc
+        return 0
+
     diffs((pc.r,))
     gq.relay()
+    gu_all.relay()
+    gq.wait_mate()
+    diffs((pc.mate, pc.xn, pc.yn))
+    gq.last()
+    gu_all.last()
+    gq.wait_mates()
     gu_all.wait_mate()
     gu_all.wait_mates()
+    diffs((pc.mate_x, pc.mate_y))
+    gq.finish()
+    diffs((pc.dg, pc.mate_d))
+    swap = pc.to_z(dif, ur.at[1], zs.at[1, 0], zr.at[1, 0])
+    swap.start()
     gu_all.finish()
-    e_user = lax.fori_loop(0, ROWS, users, jnp.zeros((D, USERS), F32))
-    egat[pc.r, row_c, :] = e_user.astype(BF16)
-    z1 = z_share(egat.at[pc.r, row_c, :], 1, 1)
-    gq.wait_mate()
-    gq.last()
-    diffs((pc.mate, pc.xn, pc.yn))
-    z1.wait()
+    lax.fori_loop(0, ROWS, users, 0)
+    for h in range(2):
+        egat[pc.r, h * D:(h + 1) * D, :] = eus[h].astype(BF16)
     ge.start()
-    gq.wait_mates()
-    gq.finish()
-    diffs((pc.mate_x, pc.mate_y, pc.dg, pc.mate_d))
-    part = pc.to_z(up.at[0, pc.zc], ur.at[0], zs.at[0, 0], zr.at[0, 0])
-    part.start()
-    ge.relay()
-    ge.last()
-    part.wait()
-    d = up[0, pc.c] + ur[0]
-    margin = jnp.sum(e_user * d, axis=0, keepdims=True)
-    soft = jnp.maximum(-margin, 0.0) + jnp.log1p(jnp.exp(-jnp.abs(margin)))
-    coef = -jax.nn.sigmoid(-margin) / BATCH
-    row8 = window(pc.c, ROWS)
-    wide = (ROWS // 2, USERS)
-    cg[pc.r, row8, :] = jnp.concatenate([jnp.broadcast_to(coef, wide), jnp.broadcast_to(soft, wide)], axis=0)
-    z3 = z_share(cg.at[pc.r, row8, :], 1, 3)
-    pi[0, pc.r, :, lane_c] = coef * d
-    z2 = z_share(pi.at[0, pc.r, :, lane_c], 1, 2)
-    gv = lane_gather(pc, pi.at[0], 2 * USERS, gs.at[4], gr.at[4])
-    gc = whole_gather(pc, cg, gs.at[5], gr.at[5])
-    z3.wait()
-    gc.start()
-    z2.wait()
-    gv.start()
+    mg[0] = pack_rows([jnp.sum(eus[h] * dif[h], axis=0, keepdims=True) for h in range(2)])
+    mz = pc.to_z(mg.at[0], mg.at[1], zs.at[1, 3], zr.at[1, 3])
+    mz.start()
     acc = pi.at[1]
     acc[:6] = jnp.zeros((6, D, SHARD), F32)
+    mz.wait()
+    margin = mg[0] + mg[1]
+    cg[pc.r, 0] = -jax.nn.sigmoid(-margin) / BATCH
+    cg[pc.r, 1] = jnp.maximum(-margin, 0.0) + jnp.log1p(jnp.exp(-jnp.abs(margin)))
+    coefs = []
+    for j in range(1, ROWS):
+        own = cg.at[pc.r]
+        coefs.append(pc.to_row(own, own, ds.at[j - 1], dr.at[j - 1], (pc.r + j) % ROWS))
+        coefs[-1].start()
+    swap.wait()
+    two = 2 * USERS
+
+    def lanes(q, h):
+        return pl.ds(pl.multiple_of((q % 2) * two + h * USERS, USERS), USERS)
+
+    def unit(q):
+        return rd.at[0, q // 2, :, window(q % 2, two)]
+
+    def unit_part(q, h):
+        return rd.at[0, q // 2, h * HALF:(h + 1) * HALF, window(q % 2, two)]
+
+    gv = Gather(pc, unit, unit_part, gs.at[4], gr.at[4])
+    for h in range(2):
+        rd[0, pc.r // 2, :, lanes(pc.r, h)] = unpack_row(cg[pc.r, 0], h) * (dif[h] + ur[1, h])
+    ge.relay()
+    gv.start()
+    ge.last()
     ge.wait_mate()
     ge.wait_mates()
     ge.finish()
-    gc.relay()
-    gc.last()
-    gc.wait_mate()
-    gc.wait_mates()
-    gc.finish()
+    for cp in coefs:
+        cp.wait()
     item_base = pc.c * ITEMS + pc.r * SHARD
 
     def item_grads(q, total):
         for h in range(2):
             k = q * 2 + h
-            co = cg[q, h * ROWS:h * ROWS + 1, :]
-            total = total + cg[q, h * ROWS + 4:h * ROWS + 5, :]
-            v = split3(co * egat[q, h * D:(h + 1) * D, :].astype(F32))
+            v = split3(unpack_row(cg[q, 0], h) * egat[q, h * D:(h + 1) * D, :].astype(F32))
             pos = ids[pl.ds(role + k, 1), :] - item_base
             neg = ids[pl.ds(2 * role + k, 1), :] - item_base
             for n in range(0, SHARD, USERS):
@@ -587,22 +619,25 @@
                 part_g = lax.dot_general(v, jnp.concatenate(picks, axis=0), NT, preferred_element_type=F32)
                 for j in range(3):
                     acc[j, :, n:n + USERS] += part_g[j * D:(j + 1) * D]
-        return total
+        return total + cg[q, 1]
 
     def user_grads(q, _):
-        for h in range(2):
-            w = split3(pi[0, q, :, h * USERS:(h + 1) * USERS])
-            pick = one_hot(ids[pl.ds(q * 2 + h, 1), :] - chunk * USERS, USERS)
-            part_g = lax.dot_general(w, pick, NT, preferred_element_type=F32)
-            for j in range(3):
-                acc[3 + j, :, :USERS] += part_g[j * D:(j + 1) * D]
+        for t in range(2):
+            w = split3(rd[0, q // 2, :, lanes(q, t)])
+            for h in range(2):
+                pick = one_hot(ids[pl.ds(q * 2 + t, 1), :] - (pc.r * 2 + h) * USERS, USERS)
+                part_g = lax.dot_general(w, pick, NT, preferred_element_type=F32)
+                for j in range(3):
+                    acc[3 + j, :, h * USERS:(h + 1) * USERS] += part_g[j * D:(j + 1) * D]
         return 0
 
-    total = lax.fori_loop(0, 4, item_grads, jnp.zeros((1, USERS), F32))
+    total = lax.fori_loop(0, 4, item_grads, jnp.zeros((ROWS, GROUP), F32))
     gv.relay()
-    total = lax.fori_loop(4, ROWS, item_grads, total)
+    total = lax.fori_loop(4, 7, item_grads, total)
     gv.last()
-    loss[...] = jnp.broadcast_to(jnp.sum(total, axis=1, keepdims=True) / BATCH, loss.shape)
+    total = lax.fori_loop(7, ROWS, item_grads, total)
+    whole = jnp.sum(jnp.sum(total, axis=0, keepdims=True), axis=1, keepdims=True)
+    loss[...] = jnp.broadcast_to(whole / BATCH, loss.shape)
     src_i, src_u = acci, accu
     src_i[...] = ((acc[0] + acc[1]) + acc[2]) / (LAYERS + 1)
     gv.wait_mate()
@@ -614,14 +649,17 @@
     xi1[pc.r] = src_i[...].astype(BF16)
     gp.start()
     lax.fori_loop(0, ROWS, user_grads, 0)
-    src_u[...] = ((acc[3, :, :USERS] + acc[4, :, :USERS]) + acc[5, :, :USERS]) / (LAYERS + 1)
-    xu[0, pc.c] = src_u[...].astype(BF16)
-    z_share(xu.at[0, pc.c], 0, 1).wait()
-
-    def back_u(k, total):
-        value = src_u[...] + total
+    for h in range(2):
+        there = slice(h * USERS, (h + 1) * USERS)
+        src_u[h] = ((acc[3, :, there] + acc[4, :, there]) + acc[5, :, there]) / (LAYERS + 1)
+        xu[0, h] = src_u[h].astype(BF16)
+
+    def back_u(k, h, total):
+        value = src_u[h] + total
         if k == LAYERS:
-            gu[...] = value
+            @pl.when(pc.c == h)
+            def _():
+                gu[...] = value
         return value.astype(BF16)
 
     def back_i(k, rows, total):
@@ -646,21 +684,17 @@
         in_specs=[hbm, vm, vm, vm],
         out_specs=(vm, vm, vm, vm, vm),
         scratch_shapes=comm_scratch() + [
-            pltpu.VMEM((SLOTS, GROUP, SHARD), i32),
-            pltpu.VMEM((2 * USERS, GROUP), i32),
-            pltpu.VMEM((ROWS, SHARD), i32),
             pltpu.VMEM((ROWS, ROWS, FOLD), i32),
             pltpu.VMEM((ROWS - 1, ROWS, ROWS, FOLD), i32),
-            pltpu.VMEM((ROWS, SHARD), F32),
             pltpu.VMEM((ROWS, 2 * USERS), i32),
             pltpu.VMEM((ROWS, 2 * USERS), i32),
-            pltpu.VMEM((2 * USERS, GROUP), F32),
-            pltpu.VMEM((D, USERS), F32),
+            pltpu.VMEM((TWO, D, USERS), F32),
             pltpu.VMEM((D, SHARD), F32),
             pltpu.VMEM((ROWS, 2 * D, USERS), BF16),
             pltpu.VMEM((ROWS, 2 * D, USERS), BF16),
-            pltpu.VMEM((ROWS, 2 * ROWS, USERS), F32),
-            dma((SLOTS,)), dma((ROWS,)), dma((ROWS,)),
+            pltpu.VMEM((ROWS, TWO, ROWS, GROUP), F32),
+            pltpu.VMEM((TWO, ROWS, GROUP), F32),
+            dma((ROWS,)), dma((ROWS,)),
         ],
         compiler_params=pltpu.CompilerParams(collective_id=0, has_side_effects=True, vmem_limit_bytes=VMEM_LIMIT),
     )(mask_blk, u0, i0, ids)

time: 284 us -> 268 us (0.944)
  Pallas kernels: 274 us -> 257 us
    pallas_call x1, Pallas kernels: 274 us -> 257 us  [mega_call(): pl.pallas_call(mega_kernel, name='mega', out_shape=(shape((D, USERS), BF1...]
where the time goes in v3:
time: 268 us; the launch traced here: 267 us
  Pallas kernels  257 us (96%)
  local copies, waits for them, and re-layouts  9.38 us (4%)
    pallas_call x1, Pallas kernels, mega_call(): pl.pallas_call(mega_kernel, name='mega', out_shape=(shape((D, USERS), BF1...  257 us
    unnamed x4, local copies, waits for them, and re-layouts  6.58 us

profile of v3, /device:TPU:0, one launch (start us, length us, event | category | flops | bytes accessed | tf_op | source)
XLA Modules:
  0.0 267.3 jit_solution(3858689232536961964)
XLA Ops:
  0.6 1.6 reshape.13.ids
  2.2 257.3 %mega.1 = (bf16[64,512]{1,0:T(8,128)(2,1)}, bf16[64,2048]{1,0:T(8,128)(2,1)}, f32[8,128]{1,0:T(8,128)}, f32[64,512]{1,0:T(8,128)}, f32[64,2048]{1,0:T(8,128)}) custom-call(s32[1024,16384]{1,0:T(8,128)} %m_hbm.1, bf16[64,512]{1,0:T(8,128)(2,1)} %bitcast.14, bf16[64,2048]{1,0:T(8,128)(2,1)} %bitcast.9, s32[48,512]{1,0:T(8,128)} %reshape.13.ids), custom_call_target="tpu_custom_call" | custom-call | tf_op jit(solution)/shard_map/mega/pallas_call | solution.py:680
  259.6 1.2 slice.3
  260.7 1.5 copy.13
  262.2 1.7 copy.14
  263.9 1.6 copy.15
  265.4 1.9 copy.16

commit v4 on v3

--- a/solution.py
+++ b/solution.py
@@ -61,12 +61,11 @@
         return pltpu.make_async_remote_copy(src_ref=src, dst_ref=dst, send_sem=ssem, recv_sem=rsem, device_id={'col': self.zc}, device_id_type=MESH)
 
 
-def entry_barrier(pc):
+def entry_signals(pc):
     bar = pltpu.get_barrier_semaphore()
-    for j in range(1, 8):
-        pl.semaphore_signal(bar, inc=1, device_id={'row': (pc.r + j) % 8}, device_id_type=MESH)
+    for j in range(1, ROWS):
+        pl.semaphore_signal(bar, inc=1, device_id={'row': (pc.r + j) % ROWS}, device_id_type=MESH)
     pl.semaphore_signal(bar, inc=1, device_id={'col': pc.zc}, device_id_type=MESH)
-    pl.semaphore_wait(bar, 8)
 
 
 class Gather:
@@ -216,36 +215,40 @@
     lax.fori_loop(0, len(shards), body, 0)
 
 
-def user_half(a, xi, up, shards, h):
+def user_quarter(a, xi, up, shards, k):
+    there = window(k % 2, FOLD)
+
     def body(j, _):
         q = choose(j, shards)
-        up[h] += lax.dot_general(xi[q], a[q, window(h, USERS), :], NT, preferred_element_type=F32)
+        up[k // 2, :, there] += lax.dot_general(xi[q], a[q, window(k, FOLD), :], NT, preferred_element_type=F32)
         return 0
 
     lax.fori_loop(0, len(shards), body, 0)
 
 
-def propagate(pc, a, xis, xus, ups, urs, scat, gath, zs, zr, fin_u, fin_i, gather_first=False):
+def propagate(pc, a, xis, xus, ups, urs, scat, gath, zs, zr, fin_u, fin_i, gather_first=False, after_u3=None):
     me = pc
     sp, sq = scat
     gp, gq = gath
     near = (me.r, me.mate, me.xn, me.yn)
     far = (me.mate_x, me.mate_y, me.dg, me.mate_d)
 
-    def swap(ch, h):
-        return me.to_z(ups[ch].at[h], urs[ch].at[h], zs.at[ch, h], zr.at[ch, h])
+    def swap(ch, k):
+        there = (k // 2, slice(None), window(k % 2, FOLD))
+        return me.to_z(ups[ch].at[there], urs[ch].at[there], zs.at[ch, k], zr.at[ch, k])
 
     def send_users(ch, shards):
-        def body(h, _):
-            user_half(a, xis[ch], ups[ch], shards, h)
-            swap(ch, h).start()
+        def body(k, _):
+            user_quarter(a, xis[ch], ups[ch], shards, k)
+            swap(ch, k).start()
             return 0
 
-        lax.fori_loop(0, 2, body, 0)
+        lax.fori_loop(0, 4, body, 0)
 
     def join_users(ch, k, xu):
         for h in range(2):
-            swap(ch, h).wait()
+            swap(ch, 2 * h).wait()
+            swap(ch, 2 * h + 1).wait()
             nxt = fin_u(k, h, ups[ch][h] + urs[ch][h])
             if xu is not None:
                 xu[h] = nxt
@@ -301,6 +304,8 @@
     gp.finish()
     send_users(0, far[2:])
     join_users(0, 3, None)
+    if after_u3 is not None:
+        after_u3()
 
     def keep3(rows, value):
         fin_i(3, rows, value)
@@ -318,7 +323,7 @@
         pltpu.VMEM((TWO, TWO, D, USERS), F32),
         pltpu.VMEM((TWO, 4, D, SHARD), F32),
         pltpu.VMEM((TWO, 6, HALF, SHARD), F32),
-        dma((5, ROWS)), dma((5, ROWS)), dma((TWO, 10)), dma((TWO, 10)), dma((TWO, 4)), dma((TWO, 4)),
+        dma((5, ROWS)), dma((5, ROWS)), dma((TWO, 10)), dma((TWO, 10)), dma((TWO, 5)), dma((TWO, 5)),
     ]
 
 
@@ -385,9 +390,7 @@
     xu[0, pc.c] = u0[...]
     acci[...] = i0[...].astype(F32)
     rowacc[...] = jnp.zeros_like(rowacc)
-    entry_barrier(pc)
-    gp.start()
-    share0 = z_share(pc, xu.at[0, pc.c], zs.at[0, 3], zr.at[0, 3])
+    entry_signals(pc)
     strip = 2 * ROWS
 
     def degree_copy(j, q):
@@ -429,17 +432,30 @@
         sums = jnp.sum(colacc[...], axis=0, keepdims=True)
         for s in range(ROWS):
             dpi[q, s:s + 1, :] = sums[:, s * FOLD:(s + 1) * FOLD]
+        return 0
+
+    def send_degrees(q):
         for j in range(1, ROWS):
             degree_copy(j, q).start()
+
+    def shard_and_send(q, _):
+        shard(q, 0)
+        send_degrees(q)
         return 0
 
-    lax.fori_loop(0, 3, shard, 0)
+    lax.fori_loop(0, 2, shard, 0)
+    pl.semaphore_wait(pltpu.get_barrier_semaphore(), ROWS)
+    gp.start()
+    share0 = z_share(pc, xu.at[0, pc.c], zs.at[0, 4], zr.at[0, 4])
+    for q in range(2):
+        send_degrees(q)
+    lax.fori_loop(2, 5, shard_and_send, 0)
     gp.relay()
-    lax.fori_loop(3, 5, shard, 0)
+    lax.fori_loop(5, 7, shard_and_send, 0)
     gp.last()
     gp.wait_mate()
     gp.wait_mates()
-    lax.fori_loop(5, ROWS, shard, 0)
+    lax.fori_loop(7, ROWS, shard_and_send, 0)
     sums = jnp.sum(rowacc[...].astype(F32).T, axis=0, keepdims=True)
     du[...] = jnp.broadcast_to(sums, du.shape).astype(jnp.int32)
     zc = pc.to_z(du, dur, ds.at[ROWS - 1], dr.at[ROWS - 1])
@@ -466,10 +482,11 @@
         def rows64(t, _):
             rows = window(t, tall)
             sub = su[rows, :]
-            for n in range(0, SHARD, GROUP):
-                col = sib[:, n:n + GROUP]
+            sub = jnp.concatenate([sub, sub], axis=1)
+            for n in range(0, SHARD, FOLD):
+                col = sib[:, n:n + FOLD]
                 both = (sub * jnp.concatenate([col] * ROWS, axis=0)).astype(BF16)
-                a[q, rows, n:n + GROUP] = a[q, rows, n:n + GROUP] * both
+                a[q, rows, n:n + FOLD] = a[q, rows, n:n + FOLD] * both
             return 0
 
         lax.fori_loop(0, 2 * USERS // tall, rows64, 0)
@@ -506,18 +523,23 @@
         acci[rows] += nxt.astype(F32)
         return nxt
 
-    role = BATCH // USERS
+    def named(role, chunk):
+        return ids[role:role + 1, window(chunk, USERS)]
+
     gu_all = whole_gather(pc, eall, gs.at[2], gr.at[2])
     ge = whole_gather(pc, egat, gs.at[3], gr.at[3])
-    propagate(fin_u=fin_u, fin_i=fin_i, **objs)
+
+    def after_u3():
+        for h in range(2):
+            eall[pc.r, h * D:(h + 1) * D, :] = (accu[h] / (LAYERS + 1)).astype(BF16)
+        gu_all.start()
+
+    propagate(fin_u=fin_u, fin_i=fin_i, after_u3=after_u3, **objs)
 
     e = (acci[...] / (LAYERS + 1)).astype(BF16)
     xi1[pc.r] = e
     gq.start()
     ei[...] = e
-    for h in range(2):
-        eall[pc.r, h * D:(h + 1) * D, :] = (accu[h] / (LAYERS + 1)).astype(BF16)
-    gu_all.start()
     eu[...] = (accu[pc.c] / (LAYERS + 1)).astype(BF16)
 
     dif, eus = up.at[0], up.at[1]
@@ -526,52 +548,57 @@
 
     def diffs(shards):
         def body(j, _):
-            q = choose(j, shards)
+            q, h = choose(j // 2, shards), j % 2
             base = pc.c * ITEMS + q * SHARD
-            for h in range(2):
-                pos = ids[pl.ds(role + pc.r * 2 + h, 1), :] - base
-                neg = ids[pl.ds(2 * role + pc.r * 2 + h, 1), :] - base
-                acc = dif[h]
-                for s in range(0, SHARD, FOLD):
-                    pick = one_hot(pos - s, FOLD) - one_hot(neg - s, FOLD)
-                    acc = acc + jnp.dot(xi1[q, :, s:s + FOLD], pick, preferred_element_type=F32)
-                dif[h] = acc
+            pos = named(1, pc.r * 2 + h) - base
+            neg = named(2, pc.r * 2 + h) - base
+            acc = dif[h]
+            for s in range(0, SHARD, FOLD):
+                pick = one_hot(pos - s, FOLD) - one_hot(neg - s, FOLD)
+                acc = acc + jnp.dot(xi1[q, :, s:s + FOLD], pick, preferred_element_type=F32)
+            dif[h] = acc
             return 0
 
-        lax.fori_loop(0, len(shards), body, 0)
-
-    def users(q, _):
-        for t in range(2):
+        lax.fori_loop(0, 2 * len(shards), body, 0)
+
+    def users(shards):
+        def body(j, _):
+            q, t = choose(j // 2, shards), j % 2
             acc = eus[t]
             for h in range(2):
-                pick = one_hot(ids[pl.ds(pc.r * 2 + t, 1), :] - (q * 2 + h) * USERS, USERS)
+                pick = one_hot(named(0, pc.r * 2 + t) - (q * 2 + h) * USERS, USERS)
                 acc = acc + jnp.dot(eall[q, h * D:(h + 1) * D, :], pick, preferred_element_type=F32)
             eus[t] = acc
-        return 0
-
+            return 0
+
+        lax.fori_loop(0, 2 * len(shards), body, 0)
+
+    gu_all.relay()
     diffs((pc.r,))
+    gu_all.wait_mate()
+    users((pc.r, pc.mate, pc.xn, pc.yn))
+    gu_all.last()
     gq.relay()
-    gu_all.relay()
+    gu_all.wait_mates()
+    gu_all.finish()
+    users((pc.mate_x, pc.mate_y, pc.dg, pc.mate_d))
+    for h in range(2):
+        egat[pc.r, h * D:(h + 1) * D, :] = eus[h].astype(BF16)
+    ge.start()
     gq.wait_mate()
     diffs((pc.mate, pc.xn, pc.yn))
     gq.last()
-    gu_all.last()
     gq.wait_mates()
-    gu_all.wait_mate()
-    gu_all.wait_mates()
     diffs((pc.mate_x, pc.mate_y))
+    ge.relay()
     gq.finish()
     diffs((pc.dg, pc.mate_d))
     swap = pc.to_z(dif, ur.at[1], zs.at[1, 0], zr.at[1, 0])
+    mg[0] = pack_rows([jnp.sum(eus[h] * dif[h], axis=0, keepdims=True) for h in range(2)])
+    mz = pc.to_z(mg.at[0], mg.at[1], zs.at[1, 4], zr.at[1, 4])
+    mz.start()
     swap.start()
-    gu_all.finish()
-    lax.fori_loop(0, ROWS, users, 0)
-    for h in range(2):
-        egat[pc.r, h * D:(h + 1) * D, :] = eus[h].astype(BF16)
-    ge.start()
-    mg[0] = pack_rows([jnp.sum(eus[h] * dif[h], axis=0, keepdims=True) for h in range(2)])
-    mz = pc.to_z(mg.at[0], mg.at[1], zs.at[1, 3], zr.at[1, 3])
-    mz.start()
+    ge.last()
     acc = pi.at[1]
     acc[:6] = jnp.zeros((6, D, SHARD), F32)
     mz.wait()
@@ -598,9 +625,7 @@
     gv = Gather(pc, unit, unit_part, gs.at[4], gr.at[4])
     for h in range(2):
         rd[0, pc.r // 2, :, lanes(pc.r, h)] = unpack_row(cg[pc.r, 0], h) * (dif[h] + ur[1, h])
-    ge.relay()
     gv.start()
-    ge.last()
     ge.wait_mate()
     ge.wait_mates()
     ge.finish()
@@ -612,8 +637,8 @@
         for h in range(2):
             k = q * 2 + h
             v = split3(unpack_row(cg[q, 0], h) * egat[q, h * D:(h + 1) * D, :].astype(F32))
-            pos = ids[pl.ds(role + k, 1), :] - item_base
-            neg = ids[pl.ds(2 * role + k, 1), :] - item_base
+            pos = named(1, k) - item_base
+            neg = named(2, k) - item_base
             for n in range(0, SHARD, USERS):
                 picks = [one_hot(pos - b, FOLD) - one_hot(neg - b, FOLD) for b in (n, n + FOLD)]
                 part_g = lax.dot_general(v, jnp.concatenate(picks, axis=0), NT, preferred_element_type=F32)
@@ -625,7 +650,7 @@
         for t in range(2):
             w = split3(rd[0, q // 2, :, lanes(q, t)])
             for h in range(2):
-                pick = one_hot(ids[pl.ds(q * 2 + t, 1), :] - (pc.r * 2 + h) * USERS, USERS)
+                pick = one_hot(named(0, q * 2 + t) - (pc.r * 2 + h) * USERS, USERS)
                 part_g = lax.dot_general(w, pick, NT, preferred_element_type=F32)
                 for j in range(3):
                     acc[3 + j, :, h * USERS:(h + 1) * USERS] += part_g[j * D:(j + 1) * D]
@@ -637,7 +662,7 @@
     gv.last()
     total = lax.fori_loop(7, ROWS, item_grads, total)
     whole = jnp.sum(jnp.sum(total, axis=0, keepdims=True), axis=1, keepdims=True)
-    loss[...] = jnp.broadcast_to(whole / BATCH, loss.shape)
+    loss[...] = whole / BATCH
     src_i, src_u = acci, accu
     src_i[...] = ((acc[0] + acc[1]) + acc[2]) / (LAYERS + 1)
     gv.wait_mate()
@@ -680,7 +705,7 @@
     return pl.pallas_call(
         mega_kernel,
         name='mega',
-        out_shape=(shape((D, USERS), BF16), shape((D, SHARD), BF16), shape((ROWS, GROUP), F32), shape((D, USERS), F32), shape((D, SHARD), F32)),
+        out_shape=(shape((D, USERS), BF16), shape((D, SHARD), BF16), shape((1, 1), F32), shape((D, USERS), F32), shape((D, SHARD), F32)),
         in_specs=[hbm, vm, vm, vm],
         out_specs=(vm, vm, vm, vm, vm),
         scratch_shapes=comm_scratch() + [
@@ -700,11 +725,21 @@
     )(mask_blk, u0, i0, ids)
 
 
+def settle_kernel(*refs):
+    half = len(refs) // 2
+    for src, dst in zip(refs[:half], refs[half:]):
+        dst[...] = src[...]
+
+
+def settle_call(*arrays):
+    shapes = tuple(jax.ShapeDtypeStruct(x.shape, x.dtype) for x in arrays)
+    return pl.pallas_call(settle_kernel, name='settle', out_shape=shapes)(*arrays)
+
+
 def solution(mesh):
     def local_fn(mask_blk, user_emb, item_emb, triples):
-        ids = triples.T.reshape(3 * BATCH // USERS, USERS)
-        eu, ei, loss, gu, gi = mega_call(mask_blk, user_emb.T, item_emb.T, ids)
-        return eu.T, ei.T, loss[0, 0], gu.T, gi.T
+        eu, ei, loss, gu, gi = settle_call(*mega_call(mask_blk, user_emb.T, item_emb.T, triples.T))
+        return eu.T, ei.T, loss.reshape(()), gu.T, gi.T
 
     user_spec = P(('row', 'col'), None)
     item_spec = P(('col', 'row'), None)

time: 268 us -> 257 us (0.959)
  local copies, waits for them, and re-layouts: 9.38 us -> 0 us
    unnamed x4 -> x0, local copies, waits for them, and re-layouts: 6.58 us -> none
    pallas_call x1, Pallas kernels: 257 us -> 254 us  [mega_call(): pl.pallas_call(mega_kernel, name='mega', out_shape=(shape((D, USERS), BF1...]
    pallas_call x0 -> x1, Pallas kernels: none -> 2.74 us  [settle_call(): pl.pallas_call(settle_kernel, name='settle', out_shape=shapes)(*arrays)]
where the time goes in v4:
time: 257 us
  Pallas kernels  257 us (100%)
    pallas_call x1, Pallas kernels, mega_call(): pl.pallas_call(mega_kernel, name='mega', out_shape=(shape((D, USERS), BF1...  254 us

profile of v4, /device:TPU:0, one launch (start us, length us, event | category | flops | bytes accessed | tf_op | source)
XLA Modules:
  0.0 257.3 jit_solution(14087930386472228185)
XLA Ops:
  0.6 253.9 %mega.1 = (bf16[64,512]{1,0:T(8,128)(2,1)}, bf16[64,2048]{1,0:T(8,128)(2,1)}, f32[1,1]{1,0:T(1,128)}, f32[64,512]{1,0:T(8,128)}, f32[64,2048]{1,0:T(8,128)}) custom-call(s32[1024,16384]{1,0:T(8,128)} %m_hbm.1, bf16[64,512]{1,0:T(8,128)(2,1)} %bitcast.10, bf16[64,2048]{1,0:T(8,128)(2,1)} %bitcast.8, s32[3,8192]{1,0:T(4,128)} %bitcast.9), custom_call_target="tpu_custom_call" | custom-call | tf_op jit(solution)/shard_map/mega/pallas_call | solution.py:705
  254.6 2.7 %settle.1 = (bf16[64,512]{1,0:T(8,128)(2,1)}, bf16[64,2048]{1,0:T(8,128)(2,1)}, f32[1,1]{1,0:T(1,128)}, f32[64,512]{1,0:T(8,128)}, f32[64,2048]{1,0:T(8,128)}) custom-call(bf16[64,512]{1,0:T(8,128)(2,1)} %get-tuple-element.15.refs_0_, bf16[64,2048]{1,0:T(8,128)(2,1)} %get-tuple-element.16.refs_1_, f32[1,1]{1,0:T(1,128)} %get-tuple-element.17.refs_2_, ...), custom_call_target="tpu_custom_call" | custom-call | tf_op jit(solution)/shard_map/settle/pallas_call | solution.py:736

commit v5 on v4

--- a/solution.py
+++ b/solution.py
@@ -590,7 +590,6 @@
     gq.last()
     gq.wait_mates()
     diffs((pc.mate_x, pc.mate_y))
-    ge.relay()
     gq.finish()
     diffs((pc.dg, pc.mate_d))
     swap = pc.to_z(dif, ur.at[1], zs.at[1, 0], zr.at[1, 0])
@@ -598,7 +597,7 @@
     mz = pc.to_z(mg.at[0], mg.at[1], zs.at[1, 4], zr.at[1, 4])
     mz.start()
     swap.start()
-    ge.last()
+    ge.relay()
     acc = pi.at[1]
     acc[:6] = jnp.zeros((6, D, SHARD), F32)
     mz.wait()
@@ -610,7 +609,7 @@
         own = cg.at[pc.r]
         coefs.append(pc.to_row(own, own, ds.at[j - 1], dr.at[j - 1], (pc.r + j) % ROWS))
         coefs[-1].start()
-    swap.wait()
+    ge.last()
     two = 2 * USERS
 
     def lanes(q, h):
@@ -623,9 +622,6 @@
         return rd.at[0, q // 2, h * HALF:(h + 1) * HALF, window(q % 2, two)]
 
     gv = Gather(pc, unit, unit_part, gs.at[4], gr.at[4])
-    for h in range(2):
-        rd[0, pc.r // 2, :, lanes(pc.r, h)] = unpack_row(cg[pc.r, 0], h) * (dif[h] + ur[1, h])
-    gv.start()
     ge.wait_mate()
     ge.wait_mates()
     ge.finish()
@@ -646,34 +642,43 @@
                     acc[j, :, n:n + USERS] += part_g[j * D:(j + 1) * D]
         return total + cg[q, 1]
 
-    def user_grads(q, _):
-        for t in range(2):
+    def user_grads(shards):
+        def body(j, _):
+            q, t = choose(j // 2, shards), j % 2
             w = split3(rd[0, q // 2, :, lanes(q, t)])
             for h in range(2):
                 pick = one_hot(named(0, q * 2 + t) - (pc.r * 2 + h) * USERS, USERS)
                 part_g = lax.dot_general(w, pick, NT, preferred_element_type=F32)
                 for j in range(3):
                     acc[3 + j, :, h * USERS:(h + 1) * USERS] += part_g[j * D:(j + 1) * D]
-        return 0
-
-    total = lax.fori_loop(0, 4, item_grads, jnp.zeros((ROWS, GROUP), F32))
+            return 0
+
+        lax.fori_loop(0, 2 * len(shards), body, 0)
+
+    total = lax.fori_loop(0, 2, item_grads, jnp.zeros((ROWS, GROUP), F32))
+    swap.wait()
+    for h in range(2):
+        rd[0, pc.r // 2, :, lanes(pc.r, h)] = unpack_row(cg[pc.r, 0], h) * (dif[h] + ur[1, h])
+    gv.start()
+    total = lax.fori_loop(2, 6, item_grads, total)
     gv.relay()
-    total = lax.fori_loop(4, 7, item_grads, total)
-    gv.last()
-    total = lax.fori_loop(7, ROWS, item_grads, total)
+    total = lax.fori_loop(6, ROWS, item_grads, total)
     whole = jnp.sum(jnp.sum(total, axis=0, keepdims=True), axis=1, keepdims=True)
     loss[...] = whole / BATCH
     src_i, src_u = acci, accu
     src_i[...] = ((acc[0] + acc[1]) + acc[2]) / (LAYERS + 1)
     gv.wait_mate()
-    gv.wait_mates()
-    gv.finish()
 
     objs['xis'], objs['gath'] = objs['xis'][::-1], objs['gath'][::-1]
     gp, gq = objs['gath']
     xi1[pc.r] = src_i[...].astype(BF16)
     gp.start()
-    lax.fori_loop(0, ROWS, user_grads, 0)
+    user_grads((pc.r, pc.mate, pc.xn, pc.yn))
+    gv.last()
+    gv.wait_mates()
+    user_grads((pc.mate_x, pc.mate_y))
+    gv.finish()
+    user_grads((pc.dg, pc.mate_d))
     for h in range(2):
         there = slice(h * USERS, (h + 1) * USERS)
         src_u[h] = ((acc[3, :, there] + acc[4, :, there]) + acc[5, :, there]) / (LAYERS + 1)

time: 257 us -> 257 us (level)
  no operation moved by 1% of the time
where the time goes in v5:
time: 257 us
  Pallas kernels  256 us (100%)
    pallas_call x1, Pallas kernels, mega_call(): pl.pallas_call(mega_kernel, name='mega', out_shape=(shape((D, USERS), BF1...  254 us

profile of v5, /device:TPU:0, one launch (start us, length us, event | category | flops | bytes accessed | tf_op | source)
XLA Modules:
  0.0 257.1 jit_solution(6646013748877887846)
XLA Ops:
  0.6 253.7 %mega.1 = (bf16[64,512]{1,0:T(8,128)(2,1)}, bf16[64,2048]{1,0:T(8,128)(2,1)}, f32[1,1]{1,0:T(1,128)}, f32[64,512]{1,0:T(8,128)}, f32[64,2048]{1,0:T(8,128)}) custom-call(s32[1024,16384]{1,0:T(8,128)} %m_hbm.1, bf16[64,512]{1,0:T(8,128)(2,1)} %bitcast.10, bf16[64,2048]{1,0:T(8,128)(2,1)} %bitcast.8, s32[3,8192]{1,0:T(4,128)} %bitcast.9), custom_call_target="tpu_custom_call" | custom-call | tf_op jit(solution)/shard_map/mega/pallas_call | solution.py:710
  254.4 2.7 %settle.1 = (bf16[64,512]{1,0:T(8,128)(2,1)}, bf16[64,2048]{1,0:T(8,128)(2,1)}, f32[1,1]{1,0:T(1,128)}, f32[64,512]{1,0:T(8,128)}, f32[64,2048]{1,0:T(8,128)}) custom-call(bf16[64,512]{1,0:T(8,128)(2,1)} %get-tuple-element.15.refs_0_, bf16[64,2048]{1,0:T(8,128)(2,1)} %get-tuple-element.16.refs_1_, f32[1,1]{1,0:T(1,128)} %get-tuple-element.17.refs_2_, ...), custom_call_target="tpu_custom_call" | custom-call | tf_op jit(solution)/shard_map/settle/pallas_call | solution.py:741
